TPU v7x, 32 devices: a 4x4x1 block of a 4x4x8 slice. The times are simulated.
32 devices in a mesh: dp: 1 (over z), m: 4 (over y), bx: 8 (over x, core).
Axes of the slice: x: 4, y: 4, z: 1, core: 2. Of those that a mesh axis runs over, the one named last changes fastest.
The devices are a block of a 4x4x8 slice.
Arguments:
- x_in: bfloat16 [24, 128, 6144], P(('dp', 'bx'), None, 'm')
- prompt_len: int32 [24], P(('dp', 'bx'))
- ln_scale: float32 [2, 6144], P(None, 'm')
- w_gate: bfloat16 [2, 6144, 8192], P(None, 'bx', 'm')
- w_up: bfloat16 [2, 6144, 8192], P(None, 'bx', 'm')
- w_q: bfloat16 [2, 6144, 48, 128], P(None, 'bx', 'm')
- w_k: bfloat16 [2, 6144, 128], P(None, 'bx')
- w_v: bfloat16 [2, 6144, 128], P(None, 'bx')
- w_down: bfloat16 [2, 8192, 6144], P(None, 'm', 'bx')
- w_o: bfloat16 [2, 48, 128, 6144], P(None, 'm', None, 'bx')
Outputs:
- output 1: bfloat16 [24, 128, 6144], P(('dp', 'bx'), None, 'm')
- output 2: bfloat16 [2, 24, 128, 128], P(None, ('dp', 'bx'))
- output 3: bfloat16 [2, 24, 128, 128], P(None, ('dp', 'bx'))
All inputs are finite; a program needn't handle non-finite values.
Results may differ from a plain program's by a relative error of at most 0.015905.
Values are sent between devices in bfloat16 or wider.
A program may use at most 768 MiB of HBM per device.

v0:
```python
import jax
import jax.numpy as jnp
from jax import lax
from jax.sharding import PartitionSpec as P

NORM_EPS = 1e-6
ROPE_BASE = 10000.0


def rotary_tables(positions, head_dim):
    half_dim = head_dim // 2
    inv_freq = ROPE_BASE ** (-jnp.arange(half_dim, dtype=jnp.float32) * (2.0 / head_dim))
    angles = positions.astype(jnp.float32)[:, None] * inv_freq[None, :]
    return jnp.cos(angles), jnp.sin(angles)


def apply_rotary(values, cos_tab, sin_tab):
    half_dim = values.shape[-1] // 2
    first_half = values[..., :half_dim]
    second_half = values[..., half_dim:]
    return jnp.concatenate([first_half * cos_tab - second_half * sin_tab, second_half * cos_tab + first_half * sin_tab], axis=-1)


def masked_attention(queries, key_rows, val_rows, query_pos, key_pos, row_lens):
    score_scale = queries.shape[-1] ** -0.5
    scores = jnp.einsum('bthd,bsd->bhts', queries, key_rows, preferred_element_type=jnp.float32) * score_scale
    visible = (key_pos[None, None, None, :] <= query_pos[None, None, :, None]) & (key_pos[None, None, None, :] < row_lens[:, None, None, None])
    scores = jnp.where(visible, scores, -1e30)
    attn_probs = jax.nn.softmax(scores, axis=-1).astype(jnp.bfloat16)
    return jnp.einsum('bhts,bsd->bhtd', attn_probs, val_rows, preferred_element_type=jnp.float32).astype(jnp.bfloat16)


def solution(mesh):
    m_size = mesh.shape['m']
    batch_axes = ('dp', 'bx')
    row_spec = P(batch_axes, None, 'm')
    cache_spec = P(None, batch_axes, None, None)
    in_specs = (row_spec, P(batch_axes), P(None, 'm'), P(None, 'bx', 'm'), P(None, 'bx', 'm'), P(None, 'bx', 'm', None), P(None, 'bx', None), P(None, 'bx', None), P(None, 'm', 'bx'), P(None, 'm', None, 'bx'))

    def device_program(x_in, prompt_len, ln_scale, w_gate, w_up, w_q, w_k, w_v, w_down, w_o):
        embed_dim = x_in.shape[2] * m_size
        positions = jnp.arange(x_in.shape[1])
        cos_tab, sin_tab = rotary_tables(positions, w_k.shape[-1])
        hidden = x_in
        k_layers = []
        v_layers = []
        for layer_idx in range(w_gate.shape[0]):
            gate_full = lax.all_gather(w_gate[layer_idx], 'bx', axis=0, tiled=True)
            up_full = lax.all_gather(w_up[layer_idx], 'bx', axis=0, tiled=True)
            query_w = lax.all_gather(w_q[layer_idx], 'bx', axis=0, tiled=True)
            key_w = lax.all_gather(w_k[layer_idx], 'bx', axis=0, tiled=True)
            value_w = lax.all_gather(w_v[layer_idx], 'bx', axis=0, tiled=True)
            down_full = lax.all_gather(w_down[layer_idx], 'bx', axis=1, tiled=True)
            out_full = lax.all_gather(w_o[layer_idx], 'bx', axis=2, tiled=True)

            hidden_f32 = hidden.astype(jnp.float32)
            moments = jnp.stack([jnp.sum(hidden_f32, axis=-1), jnp.sum(hidden_f32 * hidden_f32, axis=-1)])
            moments = lax.psum(moments, 'm')
            row_mean = (moments[0] / embed_dim)[..., None]
            row_var = (moments[1] / embed_dim)[..., None] - row_mean * row_mean
            normed_part = ((hidden_f32 - row_mean) * lax.rsqrt(row_var + NORM_EPS) * ln_scale[layer_idx]).astype(jnp.bfloat16)
            normed = lax.all_gather(normed_part, 'm', axis=2, tiled=True)

            gate_proj = jnp.einsum('bte,ef->btf', normed, gate_full, preferred_element_type=jnp.float32)
            up_proj = jnp.einsum('bte,ef->btf', normed, up_full, preferred_element_type=jnp.float32)
            act_bf = (jax.nn.silu(gate_proj) * up_proj).astype(jnp.bfloat16)
            query_lin = jnp.einsum('bte,ehd->bthd', normed, query_w, preferred_element_type=jnp.float32)
            queries = apply_rotary(query_lin, cos_tab[:, None, :], sin_tab[:, None, :]).astype(jnp.bfloat16)
            key_lin = jnp.einsum('bte,ed->btd', normed, key_w, preferred_element_type=jnp.float32)
            key_rows = apply_rotary(key_lin, cos_tab, sin_tab).astype(jnp.bfloat16)
            val_rows = jnp.einsum('bte,ed->btd', normed, value_w, preferred_element_type=jnp.float32).astype(jnp.bfloat16)
            attn_out = masked_attention(queries, key_rows, val_rows, positions, positions, prompt_len)

            partial_sum = jnp.einsum('btf,fe->bte', act_bf, down_full, preferred_element_type=jnp.float32) + jnp.einsum('bhtd,hde->bte', attn_out, out_full, preferred_element_type=jnp.float32)
            reduced = lax.psum_scatter(partial_sum.astype(jnp.bfloat16), 'm', scatter_dimension=2, tiled=True)
            hidden = (hidden_f32 + reduced.astype(jnp.float32)).astype(jnp.bfloat16)
            k_layers.append(key_rows)
            v_layers.append(val_rows)
        return hidden, jnp.stack(k_layers), jnp.stack(v_layers)

    return jax.shard_map(device_program, mesh=mesh, in_specs=in_specs, out_specs=(row_spec, cache_spec, cache_spec), check_vma=False)
```

profile of v0, /device:TPU:97, one launch (start us, length us, event | category | flops | bytes accessed | tf_op | source)
XLA Modules:
  0.0 1451.2 jit_solution(10138297571704725506)
XLA Ops:
  7.3 1.1 fusion.117
  8.4 0.8 copy.36
  9.4 1.8 convert_reduce_fusion.1
  11.1 11.2 psum.14
  22.4 1.4 fusion.37
  24.0 0.8 fusion.116
  24.9 5.0 fusion.114
  29.9 4.3 copy.37
  34.4 6.5 fusion.113
  41.0 6.6 fusion.112
  47.7 5.9 fusion.111
  53.8 5.2 fusion.115
  59.1 0.5 copy-done.16
  59.8 0.2 multiply_cosine_fusion
  60.1 27.9 %all-gather.31.cloned.1.call-done = bf16[3,128,6144]{2,1,0:T(8,128)(2,1)} async-done(((bf16[3,128,1536]{2,1,0:T(8,128)(2,1)}), bf16[3,128,6144]{2,1,0:T(8,128)(2,1)}) %all-gather.31.cloned.1.call-update) | async-done | bytes 4718608 | tf_op jit(solution)/shard_map/all_gather | solution.py:62
  88.0 4.3 fusion.52
  92.4 20.0 %all-gather.45.cloned.1.call-done = bf16[1,6144,128]{2,1,0:T(8,128)(2,1)} async-done(((bf16[1,768,128]{2,1,0:T(8,128)(2,1)}), bf16[1,6144,128]{2,1,0:T(8,128)(2,1)}) %all-gather.45.cloned.1.call-update) | async-done | bytes 1572880 | tf_op jit(solution)/shard_map/all_gather | solution.py:52
  112.4 4.2 fusion.68
  116.6 89.0 %all-gather.43.cloned.1.call-done = bf16[1,6144,12,128]{1,3,2,0:T(8,128)(2,1)} async-done(((bf16[1,768,12,128]{1,3,2,0:T(8,128)(2,1)}), bf16[1,6144,12,128]{1,3,2,0:T(8,128)(2,1)}) %all-gather.43.cloned.1.call-update) | async-done | bytes 18874384 | tf_op jit(solution)/shard_map/all_gather | solution.py:50
  205.6 14.2 fusion.20
  219.9 0.3 subtract_convert_fusion.1
  220.2 2.5 fusion.118
  222.7 103.2 %all-gather.35.cloned.1.call-done = bf16[1,6144,2048]{2,1,0:T(8,128)(2,1)} async-done(((bf16[1,768,2048]{2,1,0:T(8,128)(2,1)}), bf16[1,6144,2048]{2,1,0:T(8,128)(2,1)}) %all-gather.35.cloned.1.call-update) | async-done | bytes 25165840 | tf_op jit(solution)/shard_map/all_gather | solution.py:48
  326.0 17.3 %fusion.12 = f32[3,128,2048]{2,1,0:T(8,128)} fusion(bf16[3,128,6144]{2,1,0:T(8,128)(2,1)} %all-gather.31.cloned.1.call-done, bf16[1,6144,2048]{2,1,0:T(8,128)(2,1)} %all-gather.35.cloned.1.call-done), kind=kOutput, calls=%fused_computation.12 | convolution fusion | flops 9663676416 | bytes 33030144 | tf_op jit(solution)/shard_map/bte,ef->btf/dot_general | solution.py:64
  343.2 103.4 %all-gather.37.cloned.1.call-done = bf16[1,6144,2048]{2,1,0:T(8,128)(2,1)} async-done(((bf16[1,768,2048]{2,1,0:T(8,128)(2,1)}), bf16[1,6144,2048]{2,1,0:T(8,128)(2,1)}) %all-gather.37.cloned.1.call-update) | async-done | bytes 25165840 | tf_op jit(solution)/shard_map/all_gather | solution.py:49
  446.6 17.7 %multiply_convert_fusion.1 = bf16[3,128,2048]{2,1,0:T(8,128)(2,1)} fusion(f32[3,128,2048]{2,1,0:T(8,128)} %fusion.12, bf16[3,128,6144]{2,1,0:T(8,128)(2,1)} %all-gather.31.cloned.1.call-done, bf16[1,6144,2048]{2,1,0:T(8,128)(2,1)} %all-gather.37.cloned.1.call-done), kind=kOutput, calls=%fused_computation.37 | convolution fusion | flops 9668395008 | bytes 34603008 | tf_op jit(solution)/shard_map/bte,ef->btf/dot_general | solution.py:65
  464.3 103.1 %all-gather.39.cloned.1.call-done = bf16[1,2048,6144]{2,1,0:T(8,128)(2,1)} async-done(((bf16[1,2048,768]{2,1,0:T(8,128)(2,1)}), bf16[1,2048,6144]{2,1,0:T(8,128)(2,1)}) %all-gather.39.cloned.1.call-update) | async-done | bytes 25165840 | tf_op jit(solution)/shard_map/all_gather | solution.py:53
  567.4 17.5 %fusion.8 = f32[3,128,6144]{2,1,0:T(8,128)} fusion(bf16[3,128,2048]{2,1,0:T(8,128)(2,1)} %multiply_convert_fusion.1, bf16[1,2048,6144]{2,1,0:T(8,128)(2,1)} %all-gather.39.cloned.1.call-done), kind=kOutput, calls=%fused_computation.8 | convolution fusion | flops 9663676416 | bytes 36175872 | tf_op jit(solution)/shard_map/btf,fe->bte/dot_general | solution.py:74
  584.9 76.5 %all-gather.47.cloned.1.call-done = bf16[1,12,128,6144]{3,2,1,0:T(8,128)(2,1)} async-done(((bf16[1,12,128,768]{3,2,1,0:T(8,128)(2,1)}), bf16[1,12,128,6144]{3,2,1,0:T(8,128)(2,1)}) %all-gather.47.cloned.1.call-update) | async-done | bytes 18874384 | tf_op jit(solution)/shard_map/all_gather | solution.py:54
  661.4 16.6 %fusion.23 = bf16[3,128,6144]{2,1,0:T(8,128)(2,1)} fusion(f32[3,128,6144]{2,1,0:T(8,128)} %fusion.8, bf16[1,12,128,6144]{3,2,1,0:T(8,128)(2,1)} %all-gather.47.cloned.1.call-done, f32[3,12,128,128]{2,3,1,0:T(8,128)} %get-tuple-element.38, f32[3,12,128]{2,1,0:T(8,128)S(1)} %get-tuple-element.37, bf16[3,128,128]{2,1,0:T(8,128)(2,1)S(1)} %fusion.68), kind=kOutput, calls=%fused_computation.25 | convolution fusion | flops 7405240320 | bytes 35506176 | tf_op jit(solution)/shard_map/bhtd,hde->bte/dot_general | solution.py:74
  678.1 0.8 copy.38
  679.1 47.7 %reduce-scatter.3.cloned.1.call-done = bf16[3,128,1536]{2,1,0:T(8,128)(2,1)} async-done(((bf16[3,128,6144]{2,1,0:T(8,128)(2,1)}), bf16[3,128,1536]{2,1,0:T(8,128)(2,1)}) %reduce-scatter.3.cloned.1.call-update) | async-done | bytes 1179664 | tf_op jit(solution)/shard_map/reduce_scatter | solution.py:75
  726.8 1.8 convert_reduce_fusion
  728.7 6.9 psum.15
  735.6 1.4 fusion.42
  737.2 2.5 copy.39
  739.8 0.7 all-gather.59.cloned.1.call-update
  740.6 0.6 all-gather.49.cloned.1.call-update
  741.3 0.6 all-gather.51.cloned.1.call-update
  741.9 0.6 all-gather.53.cloned.1.call-update
  742.5 0.6 all-gather.61.cloned.1.call-update
  743.2 7.7 all-gather.55.cloned.1.call-done
  751.0 51.7 %all-gather.33.cloned.1.call-done = bf16[3,128,6144]{2,1,0:T(8,128)(2,1)} async-done(((bf16[3,128,1536]{2,1,0:T(8,128)(2,1)}), bf16[3,128,6144]{2,1,0:T(8,128)(2,1)}) %all-gather.33.cloned.1.call-update) | async-done | bytes 4718608 | tf_op jit(solution)/shard_map/all_gather | solution.py:62
  802.6 4.3 fusion.48
  807.0 89.7 %all-gather.57.cloned.1.call-done = bf16[1,6144,12,128]{1,3,2,0:T(8,128)(2,1)} async-done(((bf16[1,768,12,128]{1,3,2,0:T(8,128)(2,1)}), bf16[1,6144,12,128]{1,3,2,0:T(8,128)(2,1)}) %all-gather.57.cloned.1.call-update) | async-done | bytes 18874384 | tf_op jit(solution)/shard_map/all_gather | solution.py:50
  896.7 14.4 fusion.16
  911.2 0.3 subtract_convert_fusion
  911.5 0.4 copy-done.14
  912.0 2.3 fusion.121
  914.3 7.0 all-gather.59.cloned.1.call-done
  921.3 4.2 fusion.71
  925.5 115.7 %all-gather.49.cloned.1.call-done = bf16[1,6144,2048]{2,1,0:T(8,128)(2,1)} async-done(((bf16[1,768,2048]{2,1,0:T(8,128)(2,1)}), bf16[1,6144,2048]{2,1,0:T(8,128)(2,1)}) %all-gather.49.cloned.1.call-update) | async-done | bytes 25165840 | tf_op jit(solution)/shard_map/all_gather | solution.py:48
  1041.2 17.2 %fusion.6 = f32[3,128,2048]{2,1,0:T(8,128)} fusion(bf16[3,128,6144]{2,1,0:T(8,128)(2,1)} %all-gather.33.cloned.1.call-done, bf16[1,6144,2048]{2,1,0:T(8,128)(2,1)} %all-gather.49.cloned.1.call-done), kind=kOutput, calls=%fused_computation.6 | convolution fusion | flops 9663676416 | bytes 33030144 | tf_op jit(solution)/shard_map/bte,ef->btf/dot_general | solution.py:64
  1058.5 103.4 %all-gather.51.cloned.1.call-done = bf16[1,6144,2048]{2,1,0:T(8,128)(2,1)} async-done(((bf16[1,768,2048]{2,1,0:T(8,128)(2,1)}), bf16[1,6144,2048]{2,1,0:T(8,128)(2,1)}) %all-gather.51.cloned.1.call-update) | async-done | bytes 25165840 | tf_op jit(solution)/shard_map/all_gather | solution.py:49
  1161.8 17.8 %multiply_convert_fusion = bf16[3,128,2048]{2,1,0:T(8,128)(2,1)} fusion(f32[3,128,2048]{2,1,0:T(8,128)} %fusion.6, bf16[3,128,6144]{2,1,0:T(8,128)(2,1)} %all-gather.33.cloned.1.call-done, bf16[1,6144,2048]{2,1,0:T(8,128)(2,1)} %all-gather.51.cloned.1.call-done), kind=kOutput, calls=%fused_computation.36 | convolution fusion | flops 9668395008 | bytes 34603008 | tf_op jit(solution)/shard_map/bte,ef->btf/dot_general | solution.py:65
  1179.6 102.9 %all-gather.53.cloned.1.call-done = bf16[1,2048,6144]{2,1,0:T(8,128)(2,1)} async-done(((bf16[1,2048,768]{2,1,0:T(8,128)(2,1)}), bf16[1,2048,6144]{2,1,0:T(8,128)(2,1)}) %all-gather.53.cloned.1.call-update) | async-done | bytes 25165840 | tf_op jit(solution)/shard_map/all_gather | solution.py:53
  1282.5 17.3 %fusion.2 = f32[3,128,6144]{2,1,0:T(8,128)} fusion(bf16[3,128,2048]{2,1,0:T(8,128)(2,1)} %multiply_convert_fusion, bf16[1,2048,6144]{2,1,0:T(8,128)(2,1)} %all-gather.53.cloned.1.call-done), kind=kOutput, calls=%fused_computation.2 | convolution fusion | flops 9663676416 | bytes 36175872 | tf_op jit(solution)/shard_map/btf,fe->bte/dot_general | solution.py:74
  1299.8 76.6 %all-gather.61.cloned.1.call-done = bf16[1,12,128,6144]{3,2,1,0:T(8,128)(2,1)} async-done(((bf16[1,12,128,768]{3,2,1,0:T(8,128)(2,1)}), bf16[1,12,128,6144]{3,2,1,0:T(8,128)(2,1)}) %all-gather.61.cloned.1.call-update) | async-done | bytes 18874384 | tf_op jit(solution)/shard_map/all_gather | solution.py:54
  1376.3 16.4 %fusion.22 = bf16[3,128,6144]{2,1,0:T(8,128)(2,1)} fusion(f32[3,128,6144]{2,1,0:T(8,128)} %fusion.2, bf16[1,12,128,6144]{3,2,1,0:T(8,128)(2,1)} %all-gather.61.cloned.1.call-done, f32[3,12,128,128]{2,3,1,0:T(8,128)} %get-tuple-element.40, f32[3,12,128]{2,1,0:T(8,128)S(1)} %get-tuple-element.39, bf16[3,128,128]{2,1,0:T(8,128)(2,1)S(1)} %fusion.71), kind=kOutput, calls=%fused_computation.23 | convolution fusion | flops 7405240320 | bytes 35506176 | tf_op jit(solution)/shard_map/bhtd,hde->bte/dot_general | solution.py:74
  1392.8 0.7 copy-done.10
  1393.6 0.8 copy.21
  1394.4 0.7 pad_maximum_fusion
  1395.1 46.5 %reduce-scatter.5.cloned.1.call-done = bf16[3,128,1536]{2,1,0:T(8,128)(2,1)} async-done(((bf16[3,128,6144]{2,1,0:T(8,128)(2,1)}), bf16[3,128,1536]{2,1,0:T(8,128)(2,1)}) %reduce-scatter.5.cloned.1.call-update) | async-done | bytes 1179664 | tf_op jit(solution)/shard_map/reduce_scatter | solution.py:75
  1441.6 2.6 fusion.43
  (78 shorter events, 2.3 us)
Async XLA Ops:
  7.2 15.3 %copy-start = (bf16[3,128,1536]{2,1,0:T(8,128)(2,1)S(1)}, bf16[3,128,1536]{2,1,0:T(8,128)(2,1)}, u32[]{:S(2)}) copy-start(bf16[3,128,1536]{2,1,0:T(8,128)(2,1)} %param.10) | copy-start | bytes 3538948
  7.2 15.2 %copy-start.15 = (f32[2,1536]{1,0:T(2,128)S(1)}, f32[2,1536]{1,0:T(2,128)}, u32[]{:S(2)}) copy-start(f32[2,1536]{1,0:T(2,128)} %param.12) | copy-start | bytes 36868
  7.2 52.9 %all-gather.41.cloned.1.call-start = ((), (), s32[]{:S(2)}) async-start(), calls=%async_computation.9 | async-start | bytes 1769472 | tf_op jit(solution)/shard_map/all_gather | solution.py:51
  9.3 14.7 %copy-start.6 = (bf16[2,768,128]{2,1,0:T(8,128)(2,1)S(1)}, bf16[2,768,128]{2,1,0:T(8,128)(2,1)}, u32[]{:S(2)}) copy-start(bf16[2,768,128]{2,1,0:T(8,128)(2,1)} %param.17) | copy-start | bytes 1179652
  9.3 78.7 %all-gather.31.cloned.1.call-start = ((), (), s32[]{:S(2)}) async-start(), calls=%async_computation.2 | async-start | bytes 5898240 | tf_op jit(solution)/shard_map/all_gather | solution.py:62
  23.9 88.5 %all-gather.45.cloned.1.call-start = ((), (), s32[]{:S(2)}) async-start(), calls=%async_computation.11 | async-start | bytes 1769472 | tf_op jit(solution)/shard_map/all_gather | solution.py:52
  24.9 180.8 %all-gather.43.cloned.1.call-start = ((), (), s32[]{:S(2)}) async-start(), calls=%async_computation.10 | async-start | bytes 21233664 | tf_op jit(solution)/shard_map/all_gather | solution.py:50
  34.3 291.7 %all-gather.35.cloned.1.call-start = ((), (), s32[]{:S(2)}) async-start(), calls=%async_computation.6 | async-start | bytes 28311552 | tf_op jit(solution)/shard_map/all_gather | solution.py:48
  41.0 405.6 %all-gather.37.cloned.1.call-start = ((), (), s32[]{:S(2)}) async-start(), calls=%async_computation.7 | async-start | bytes 28311552 | tf_op jit(solution)/shard_map/all_gather | solution.py:49
  47.7 519.7 %all-gather.39.cloned.1.call-start = ((), (), s32[]{:S(2)}) async-start(), calls=%async_computation.8 | async-start | bytes 28311552 | tf_op jit(solution)/shard_map/all_gather | solution.py:53
  53.7 607.7 %all-gather.47.cloned.1.call-start = ((), (), s32[]{:S(2)}) async-start(), calls=%async_computation.12 | async-start | bytes 21233664 | tf_op jit(solution)/shard_map/all_gather | solution.py:54
  59.0 0.7 copy-start.16
  59.0 667.8 %reduce-scatter.3.cloned.1.call-start = ((), (), s32[]{:S(2)}) async-start(), calls=%async_computation.3 | async-start | bytes 5898240 | tf_op jit(solution)/shard_map/reduce_scatter | solution.py:75
  59.8 160.4 %copy-start.13 = (pred[3,128,128]{1,2,0:T(8,128)(4,1)}, pred[3,128,128]{1,2,0:T(8,128)(4,1)S(1)}, u32[]{:S(2)}) copy-start(pred[3,128,128]{1,2,0:T(8,128)(4,1)S(1)} %broadcast_and_fusion) | copy-start | bytes 147460
  60.0 159.8 %copy-start.2 = (f32[128,64]{0,1:T(8,128)}, f32[128,64]{0,1:T(8,128)S(1)}, u32[]{:S(2)}) copy-start(f32[128,64]{0,1:T(8,128)S(1)} %get-tuple-element.35) | copy-start | bytes 98308
  60.0 159.8 %copy-start.4 = (f32[128,64]{0,1:T(8,128)}, f32[128,64]{0,1:T(8,128)S(1)}, u32[]{:S(2)}) copy-start(f32[128,64]{0,1:T(8,128)S(1)} %get-tuple-element.36) | copy-start | bytes 98308
  92.4 127.9 %copy-start.9 = (bf16[3,128,64]{1,2,0:T(8,128)(2,1)}, bf16[3,128,64]{1,2,0:T(8,128)(2,1)S(1)}, u32[]{:S(2)}) copy-start(bf16[3,128,64]{1,2,0:T(8,128)(2,1)S(1)} %get-tuple-element.33) | copy-start | bytes 147460
  92.4 127.9 %copy-start.11 = (bf16[3,128,64]{1,2,0:T(8,128)(2,1)}, bf16[3,128,64]{1,2,0:T(8,128)(2,1)S(1)}, u32[]{:S(2)}) copy-start(bf16[3,128,64]{1,2,0:T(8,128)(2,1)S(1)} %get-tuple-element.34) | copy-start | bytes 147460
  116.6 544.8 %copy-start.7 = (bf16[3,128,128]{2,1,0:T(8,128)(2,1)}, bf16[3,128,128]{2,1,0:T(8,128)(2,1)S(1)}, u32[]{:S(2)}) copy-start(bf16[3,128,128]{2,1,0:T(8,128)(2,1)S(1)} %fusion.68) | copy-start | bytes 294916
  678.1 72.9 %all-gather.55.cloned.1.call-start = ((), (), s32[]{:S(2)}) async-start(), calls=%async_computation.16 | async-start | bytes 1769472 | tf_op jit(solution)/shard_map/all_gather | solution.py:51
  679.0 123.6 %all-gather.33.cloned.1.call-start = ((), (), s32[]{:S(2)}) async-start(), calls=%async_computation.4 | async-start | bytes 5898240 | tf_op jit(solution)/shard_map/all_gather | solution.py:62
  728.7 8.5 copy-start.1
  737.1 159.6 %all-gather.57.cloned.1.call-start = ((), (), s32[]{:S(2)}) async-start(), calls=%async_computation.17 | async-start | bytes 21233664 | tf_op jit(solution)/shard_map/all_gather | solution.py:50
  739.7 181.6 %all-gather.59.cloned.1.call-start = ((), (), s32[]{:S(2)}) async-start(), calls=%async_computation.18 | async-start | bytes 1769472 | tf_op jit(solution)/shard_map/all_gather | solution.py:52
  740.5 300.7 %all-gather.49.cloned.1.call-start = ((), (), s32[]{:S(2)}) async-start(), calls=%async_computation.13 | async-start | bytes 28311552 | tf_op jit(solution)/shard_map/all_gather | solution.py:48
  741.2 420.6 %all-gather.51.cloned.1.call-start = ((), (), s32[]{:S(2)}) async-start(), calls=%async_computation.14 | async-start | bytes 28311552 | tf_op jit(solution)/shard_map/all_gather | solution.py:49
  741.8 540.6 %all-gather.53.cloned.1.call-start = ((), (), s32[]{:S(2)}) async-start(), calls=%async_computation.15 | async-start | bytes 28311552 | tf_op jit(solution)/shard_map/all_gather | solution.py:53
  742.5 633.9 %all-gather.61.cloned.1.call-start = ((), (), s32[]{:S(2)}) async-start(), calls=%async_computation.19 | async-start | bytes 21233664 | tf_op jit(solution)/shard_map/all_gather | solution.py:54
  743.1 63.9 %copy-start.3 = (f32[128,64]{0,1:T(8,128)S(1)}, f32[128,64]{0,1:T(8,128)}, u32[]{:S(2)}) copy-start(f32[128,64]{0,1:T(8,128)} %copy-done.2) | copy-start | bytes 98308
  743.1 63.9 %copy-start.5 = (f32[128,64]{0,1:T(8,128)S(1)}, f32[128,64]{0,1:T(8,128)}, u32[]{:S(2)}) copy-start(f32[128,64]{0,1:T(8,128)} %copy-done.4) | copy-start | bytes 98308
  743.1 698.5 %reduce-scatter.5.cloned.1.call-start = ((), (), s32[]{:S(2)}) async-start(), calls=%async_computation.5 | async-start | bytes 5898240 | tf_op jit(solution)/shard_map/reduce_scatter | solution.py:75
  911.2 0.8 copy-start.14
  1392.8 0.8 copy-start.10
  1392.8 0.8 copy-start.12
  1392.8 1.7 copy-start.8
Sparse Core Ops, SparseCore 0:
  10.2 26.0 all-gather.40
  38.4 49.4 all-gather.30
  89.6 22.7 all-gather.44
  113.9 91.7 all-gather.42
  207.1 118.8 all-gather.34
  327.4 119.1 all-gather.36
  448.2 119.1 all-gather.38
  569.0 92.3 all-gather.46
  678.2 48.6 reduce-scatter.2
  728.9 22.0 all-gather.54
  753.1 49.4 all-gather.32
  804.1 92.5 all-gather.56
  898.9 22.3 all-gather.58
  922.7 118.4 all-gather.48
  1042.7 119.1 all-gather.50
  1163.3 119.1 all-gather.52
  1283.9 92.3 all-gather.60
  1393.0 48.6 reduce-scatter.4
where the time goes:
time: 1460 us; the launch traced here: 1450 us
  waiting for transfers between devices  1180 us (81%)
  matrix products  188 us (13%)
  local copies, waits for them, and re-layouts  42.1 us (3%)
  blocking collectives  18.1 us (1%)
  between operations  14.9 us (1%)
    all_gather x2, waiting for transfers between devices, device_program(): gate_full = lax.all_gather(w_gate[layer_idx], 'bx', axis=0, tiled=True)  219 us
    all_gather x2, waiting for transfers between devices, device_program(): up_full = lax.all_gather(w_up[layer_idx], 'bx', axis=0, tiled=True)  207 us
    all_gather x2, waiting for transfers between devices, device_program(): down_full = lax.all_gather(w_down[layer_idx], 'bx', axis=1, tiled=True)  206 us
    all_gather x2, waiting for transfers between devices, device_program(): query_w = lax.all_gather(w_q[layer_idx], 'bx', axis=0, tiled=True)  179 us
    all_gather x2, waiting for transfers between devices, device_program(): out_full = lax.all_gather(w_o[layer_idx], 'bx', axis=2, tiled=True)  153 us
    reduce_scatter x2, waiting for transfers between devices, device_program(): lax.psum_scatter(partial_sum.astype(jnp.bfloat16), 'm', scatter_dimension...  94.2 us
    all_gather x2, waiting for transfers between devices, device_program(): normed = lax.all_gather(normed_part, 'm', axis=2, tiled=True)  79.6 us
    dot_general x2, matrix products, device_program(): jnp.einsum('bte,ef->btf', normed, up_full, preferred_element_type=jnp.flo...  35.4 us
  transfers between devices with their start and end apart: 18, of which 17 were waited for; matrix products, arithmetic and copies ran while one was open for 14% of the time, Pallas kernels for 0%

commit v1 on v0

v1 whole, which is shorter than its diff:
```python
import functools

import jax
import jax.numpy as jnp
from jax import lax
from jax.experimental import pallas as pl
from jax.experimental.pallas import tpu as pltpu
from jax.sharding import PartitionSpec as P


NORM_EPS = 1e-6
ROPE_BASE = 10000.0


def rotary_tables(positions, head_dim):
    half_dim = head_dim // 2
    inv_freq = ROPE_BASE ** (-jnp.arange(half_dim, dtype=jnp.float32) * (2.0 / head_dim))
    angles = positions.astype(jnp.float32)[:, None] * inv_freq[None, :]
    return jnp.cos(angles), jnp.sin(angles)


def up_kernel(head_dim, order_ref, lens_ref, mine_ref, other_ref, scale_ref, cos_ref, sin_ref, *refs):
    weights, (both_ref, k_ref, v_ref, h_ref, q_ref, keys_ref, vals_ref, wg_ref, wu_ref, wq_ref, wv_ref, sems) = refs[:16], refs[16:]
    copies = []
    for i, (group, dst) in enumerate(zip((weights[0:4], weights[4:8], weights[8:12], weights[12:16]), (wg_ref, wu_ref, wq_ref, wv_ref))):
        for p, src in enumerate(group):
            if dst is wq_ref:
                for h in range(src.shape[0]):
                    copies.append(pltpu.make_async_copy(src.at[h], dst.at[p, :, pl.ds(h * head_dim, head_dim)], sems.at[i, p]))
            else:
                copies.append(pltpu.make_async_copy(src, dst.at[p], sems.at[i, p]))
    for copy in copies:
        copy.start()

    blocks, half_rows, feat = mine_ref.shape
    embed_dim = blocks * feat
    part = feat // 2
    step = 16

    def norm(i, carry):
        rows = pl.ds(pl.multiple_of(i * step, step), step)
        for src, base in ((mine_ref, 0), (other_ref, half_rows)):
            xs = [src[e, rows, :].astype(jnp.float32) for e in range(blocks)]
            mean = sum(jnp.sum(x, axis=-1, keepdims=True) for x in xs) / embed_dim
            xs = [x - mean for x in xs]
            var = sum(jnp.sum(x * x, axis=-1, keepdims=True) for x in xs) / embed_dim
            inv = lax.rsqrt(var + NORM_EPS)
            out_rows = pl.ds(pl.multiple_of(base + i * step, step), step)
            for e in range(blocks):
                y = (xs[e] * inv * scale_ref[e:e + 1, :]).astype(jnp.bfloat16)
                h_ref[2 * e, out_rows, :] = y[:, :part]
                h_ref[2 * e + 1, out_rows, :] = y[:, part:]
        return carry

    lax.fori_loop(0, half_rows // step, norm, 0)
    for copy in copies:
        copy.wait()

    n_parts = 2 * blocks
    order = [order_ref[p] for p in range(n_parts)]
    tile = 256
    f_cols = wg_ref.shape[-1]
    n_heads = wq_ref.shape[-1] // head_dim
    half_dim = head_dim // 2

    def product(rows, w_ref, cols):
        total = None
        for p in range(n_parts):
            w = w_ref[p // 2, pl.ds((p % 2) * part, part), cols]
            term = jnp.dot(h_ref[order[p], rows, :], w, preferred_element_type=jnp.float32)
            total = term if total is None else total + term
        return total

    def project(r, carry):
        rows = pl.ds(pl.multiple_of(r * tile, tile), tile)
        for n in range(0, f_cols, tile):
            cols = pl.ds(n, tile)
            gate = product(rows, wg_ref, cols)
            up = product(rows, wu_ref, cols)
            both_ref[rows, cols] = (gate * (1.0 / (1.0 + jnp.exp(-gate))) * up).astype(jnp.bfloat16)
        cos_t = jnp.concatenate([cos_ref[...]] * (tile // cos_ref.shape[0]), axis=0)
        sin_t = jnp.concatenate([sin_ref[...]] * (tile // sin_ref.shape[0]), axis=0)
        rotary = lambda u: (u * cos_t + pltpu.roll(u, half_dim, 1) * sin_t).astype(jnp.bfloat16)
        kv = product(rows, wv_ref, pl.ds(0, 2 * head_dim))
        keys_ref[rows, :] = rotary(kv[:, :head_dim])
        vals_ref[rows, :] = kv[:, head_dim:].astype(jnp.bfloat16)
        query = product(rows, wq_ref, pl.ds(0, n_heads * head_dim))
        for h in range(n_heads):
            cols = slice(h * head_dim, (h + 1) * head_dim)
            q_ref[rows, cols] = rotary(query[:, cols])
        return carry

    lax.fori_loop(0, h_ref.shape[1] // tile, project, 0)
    seq = cos_ref.shape[0]
    k_ref[...] = keys_ref[:seq, :]
    v_ref[...] = vals_ref[:seq, :]
    row_id = lax.broadcasted_iota(jnp.int32, (seq, seq), 0)
    col_id = lax.broadcasted_iota(jnp.int32, (seq, seq), 1)

    def attend(b, carry):
        rows = pl.ds(pl.multiple_of(b * seq, seq), seq)
        keys, vals = keys_ref[rows, :], vals_ref[rows, :]
        visible = (col_id <= row_id) & (col_id < lens_ref[b])
        for h in range(n_heads):
            query = q_ref[rows, h * head_dim:(h + 1) * head_dim]
            scores = lax.dot_general(query, keys, (((1,), (1,)), ((), ())), preferred_element_type=jnp.float32) * (head_dim ** -0.5)
            scores = jnp.where(visible, scores, -1e30)
            weight = jnp.exp(scores - jnp.max(scores, axis=-1, keepdims=True))
            probs = (weight / jnp.sum(weight, axis=-1, keepdims=True)).astype(jnp.bfloat16)
            out = jnp.dot(probs, vals, preferred_element_type=jnp.float32)
            both_ref[rows, f_cols + h * head_dim:f_cols + (h + 1) * head_dim] = out.astype(jnp.bfloat16)
        return carry

    lax.fori_loop(0, h_ref.shape[1] // seq, attend, 0)


def down_kernel(order_ref, both_ref, *refs):
    weights, (keep_ref, send_ref, w_ref, sems) = refs[:8], refs[8:]
    pieces = w_ref.shape[0]
    copies = []
    for p in range(pieces):
        depth = weights[p].shape[0]
        copies.append((
            pltpu.make_async_copy(weights[p], w_ref.at[p, pl.ds(0, depth), :], sems.at[0, p]),
            pltpu.make_async_copy(weights[pieces + p], w_ref.at[p, pl.ds(depth, weights[pieces + p].shape[0]), :], sems.at[1, p]),
        ))
    for pair in copies:
        for copy in pair:
            copy.start()
    half_rows = keep_ref.shape[1]
    part = w_ref.shape[-1] // 2
    tile = 256
    for p in range(pieces):
        for copy in copies[p]:
            copy.wait()
        for j in range(2):
            block = order_ref[2 * p + j]
            for n in range(0, part, tile):
                w = w_ref[p, :, j * part + n:j * part + n + tile]
                cols = pl.ds(pl.multiple_of(lax.rem(block, 2) * part + n, 128), tile)
                for dst, base in ((send_ref, half_rows), (keep_ref, 0)):
                    out = jnp.dot(both_ref[base:base + half_rows, :], w, preferred_element_type=jnp.float32)
                    dst[lax.div(block, 2), :, cols] = out.astype(jnp.bfloat16)


def up_call(order, lens, mine, other, scale, cos_t, sin_t, gate, up, query, kv):
    blocks, half_rows, feat = mine.shape
    rows = 2 * half_rows
    head_dim = cos_t.shape[-1]
    f_cols, heads = gate[0].shape[-1], query[0].shape[0]
    wide = f_cols + heads * head_dim
    n_all = 2 * f_cols + (heads + 2) * head_dim
    vmem, smem, hbm = (pl.BlockSpec(memory_space=space) for space in (pltpu.VMEM, pltpu.SMEM, pltpu.HBM))
    bf16 = jnp.bfloat16
    return pl.pallas_call(
        functools.partial(up_kernel, head_dim),
        out_shape=(jax.ShapeDtypeStruct((rows, wide), bf16), jax.ShapeDtypeStruct(cos_t.shape, bf16), jax.ShapeDtypeStruct(cos_t.shape, bf16)),
        in_specs=[smem, smem] + [vmem] * 5 + [hbm] * 16,
        out_specs=(vmem, vmem, vmem),
        scratch_shapes=[
            pltpu.VMEM((2 * blocks, rows, feat // 2), bf16),
            pltpu.VMEM((rows, heads * head_dim), bf16),
            pltpu.VMEM((rows, head_dim), bf16),
            pltpu.VMEM((rows, head_dim), bf16),
            pltpu.VMEM((blocks, feat, f_cols), bf16),
            pltpu.VMEM((blocks, feat, f_cols), bf16),
            pltpu.VMEM((blocks, feat, heads * head_dim), bf16),
            pltpu.VMEM((blocks, feat, 2 * head_dim), bf16),
            pltpu.SemaphoreType.DMA((4, blocks)),
        ],
        compiler_params=pltpu.CompilerParams(vmem_limit_bytes=60 << 20),
        cost_estimate=pl.CostEstimate(flops=2 * rows * blocks * feat * n_all, bytes_accessed=2 * blocks * feat * (n_all + rows), transcendentals=0),
    )(order, lens, mine, other, scale, cos_t, sin_t, *gate, *up, *query, *kv)


def down_call(order, both, down, out_w):
    rows, wide = both.shape
    pieces, feat = len(down), down[0].shape[-1]
    vmem, smem, hbm = (pl.BlockSpec(memory_space=space) for space in (pltpu.VMEM, pltpu.SMEM, pltpu.HBM))
    shape = jax.ShapeDtypeStruct((pieces, rows // 2, feat), jnp.bfloat16)
    return pl.pallas_call(
        down_kernel,
        out_shape=(shape, shape),
        in_specs=[smem, vmem] + [hbm] * (2 * pieces),
        out_specs=(vmem, vmem),
        scratch_shapes=[pltpu.VMEM((pieces, wide, feat), jnp.bfloat16), pltpu.SemaphoreType.DMA((2, pieces))],
        compiler_params=pltpu.CompilerParams(vmem_limit_bytes=48 << 20),
        cost_estimate=pl.CostEstimate(flops=2 * rows * wide * pieces * feat, bytes_accessed=2 * pieces * feat * (wide + rows), transcendentals=0),
    )(order, both, *down, *out_w)


class Pairing:
    def __init__(self, bx_size, first):
        chips = bx_size // 2
        self.partner = [0] * chips
        for low in range(first, first + chips, 2):
            a, b = low % chips, (low + 1) % chips
            self.partner[a], self.partner[b] = b, a
        self.perm = [(2 * c + k, 2 * self.partner[c] + k) for c in range(chips) for k in range(2)]

    def send(self, value):
        return lax.ppermute(value, 'bx', self.perm)


def solution(mesh):
    bx_size = mesh.shape['bx']
    batch_axes = ('dp', 'bx')
    row_spec = P(batch_axes, None, 'm')
    cache_spec = P(None, batch_axes, None, None)
    in_specs = (row_spec, P(batch_axes), P(None, 'm'), P(None, 'bx', 'm'), P(None, 'bx', 'm'), P(None, 'bx', 'm', None), P(None, 'bx', None), P(None, 'bx', None), P(None, 'm', 'bx'), P(None, 'm', None, 'bx'))
    pairings = (Pairing(bx_size, 0), Pairing(bx_size, 1))
    core_perm = [(i, i ^ 1) for i in range(bx_size)]

    def swap_core(value):
        return lax.ppermute(value, 'bx', core_perm)

    def device_program(x_in, prompt_len, ln_scale, w_gate, w_up, w_q, w_k, w_v, w_down, w_o):
        rows, seq, _ = x_in.shape
        head_dim = w_k.shape[-1]
        me = lax.axis_index('bx').astype(jnp.uint32)
        chip, core = me >> 1, me & 1
        positions = jnp.arange(seq)
        cos_tab, sin_tab = rotary_tables(positions, head_dim)
        cos_full = jnp.concatenate([cos_tab, cos_tab], axis=1)
        sin_full = jnp.concatenate([-sin_tab, sin_tab], axis=1)
        scale_all = lax.all_gather(ln_scale, 'm', axis=0)
        layers = w_gate.shape[0]
        heads = w_q.shape[2]

        def spread(w, e_axis, layer, same_col, same_row, c_index):
            f_axis = 1 - e_axis
            half = w.shape[1 + f_axis] // 2
            quarter = half // 2

            def take(at, size):
                starts, sizes = [jnp.uint32(layer), jnp.uint32(0), jnp.uint32(0)], list(w.shape[1:3])
                starts[1 + f_axis], sizes[f_axis] = at * size, size
                tail = w.shape[3:]
                starts += [jnp.uint32(0)] * len(tail)
                return lax.dynamic_slice(w, starts, [1] + sizes + list(tail))[0]

            other = swap_core(take(1 - core, half))
            other_at = lambda i: lax.dynamic_slice_in_dim(other, i * quarter, quarter, f_axis)
            mine_c = jnp.concatenate([take(2 * core + c_index, quarter), other_at(c_index)], axis=e_axis)
            other_c = jnp.concatenate([take(2 * core + (1 - c_index), quarter), other_at(1 - c_index)], axis=e_axis)
            from_row = same_row.send(other_c)
            return [mine_c, from_row, same_col.send(mine_c), same_col.send(from_row)]

        def spread_kv(w, same_col, same_row):
            from_row = same_row.send(w)
            mine = jnp.stack([w, from_row, same_col.send(w), same_col.send(from_row)])
            full = jnp.concatenate([mine, swap_core(mine)], axis=1)
            return [full[i] for i in range(4)]

        plans = []
        for layer in range(layers):
            same_col = pairings[layer % 2]
            same_row = pairings[(layer + 1) % 2]
            flipped = layer % 2
            c_index = ((chip + flipped) >> 1) & 1
            owners = tuple(chip ^ mask for mask in ((0, 3, 1, 2), (0, 1, 3, 2))[flipped])
            order = jnp.stack([2 * owner + (core ^ j) for owner in owners for j in range(2)]).astype(jnp.int32)
            args = (same_col, same_row, c_index)
            gate = spread(w_gate, 0, layer, *args)
            up = spread(w_up, 0, layer, *args)
            query_w = spread(jnp.swapaxes(w_q, 1, 2), 1, layer, *args)
            kv_w = spread_kv(jnp.concatenate([w_k[layer], w_v[layer]], axis=1), same_col, same_row)
            down = spread(w_down, 1, layer, *args)
            out_w = spread(w_o.reshape(layers, heads * head_dim, w_o.shape[-1]), 1, layer, *args)
            lens = jnp.stack([prompt_len, same_row.send(prompt_len)])
            lens = jnp.stack([lens, swap_core(lens)])
            plans.append((same_row, order, lens, gate, up, query_w, kv_w, down, out_w))

        hidden = [lax.optimization_barrier(x_in[c]) for c in range(rows)]
        k_layers = []
        v_layers = []
        for layer in range(layers):
            same_row, order, lens, gate, up, query_w, kv_w, down, out_w = plans[layer]
            k_rows, v_rows, following = [], [], []
            for c in range(rows):
                shared = same_row.send(hidden[c])
                pair = jnp.concatenate([hidden[c], shared], axis=0)
                mine = lax.all_gather(pair, 'm', axis=0)
                other = swap_core(mine)
                both, key_rows, val_rows = up_call(order, lens[:, :, c].reshape(-1), mine, other, scale_all[:, layer], cos_full, sin_full, gate, up, query_w, kv_w)
                k_rows.append(key_rows)
                v_rows.append(val_rows)
                keep, send = down_call(order, both, down, out_w)
                from_core = swap_core(send)
                ordered = (keep.astype(jnp.float32) + from_core.astype(jnp.float32)).astype(jnp.bfloat16)
                reduced = lax.psum_scatter(ordered, 'm', scatter_dimension=0)
                from_row = same_row.send(reduced[seq:])
                following.append((hidden[c].astype(jnp.float32) + (reduced[:seq].astype(jnp.float32) + from_row.astype(jnp.float32))).astype(jnp.bfloat16))
            hidden = following
            k_layers.append(jnp.stack(k_rows))
            v_layers.append(jnp.stack(v_rows))
        return jnp.stack(hidden), jnp.stack(k_layers), jnp.stack(v_layers)

    return jax.shard_map(device_program, mesh=mesh, in_specs=in_specs, out_specs=(row_spec, cache_spec, cache_spec), check_vma=False)
```

time: 1460 us -> 1160 us (0.79)
  waiting for transfers between devices: 1180 us -> 656 us
  Pallas kernels: 0 us -> 235 us
  matrix products: 188 us -> 0 us
  starting transfers between devices: 1.15 us -> 76.7 us
  other arithmetic: 10.9 us -> 81.4 us
  local copies, waits for them, and re-layouts: 42.1 us -> 72.5 us
    all_gather x16 -> x6, waiting for transfers between devices: 1080 us -> 0.03 us  [device_program(): mine = lax.all_gather(pair, 'm', axis=0)]
    ppermute x0 -> x76, waiting for transfers between devices: none -> 624 us  [the longest x50 590 us: send(): return lax.ppermute(value, 'bx', self.perm)]
    pallas_call x0 -> x12, Pallas kernels: none -> 235 us  [the longest x6 164 us: up_call(): pl.pallas_call(functools.partial(up_kernel, head_dim), out_shape=(jax.Sha...]
    dot_general x14 -> x0, matrix products: 184 us -> none  [the longest x2 35.4 us: device_program(): jnp.einsum('bte,ef->btf', normed, up_full, preferred_element_type=jnp.flo...]
    ppermute x0 -> x76, starting transfers between devices: none -> 74.4 us  [the longest x50 47.5 us: send(): return lax.ppermute(value, 'bx', self.perm)]
    reduce_scatter x2 -> x6, waiting for transfers between devices: 94.2 us -> 31.9 us  [device_program(): reduced = lax.psum_scatter(ordered, 'm', scatter_dimension=0)]
    concatenate x0 -> x29, other arithmetic: none -> 38.5 us  [the longest x10 13.9 us: spread(): jnp.concatenate([take(2 * core + c_index, quarter), other_at(c_index)], a...]
    squeeze x0 -> x14, local copies, waits for them, and re-layouts: none -> 33.6 us  [the longest x10 28.1 us: take(): return lax.dynamic_slice(w, starts, [1] + sizes + list(tail))[0]]
  transfers between devices with their start and end apart: 18 -> 88, of which waited for: 17 -> 34; matrix products, arithmetic and copies ran while one was open for 14% -> 12% of each run, Pallas kernels for 0% -> 20%
where the time goes in v1:
time: 1160 us; the launch traced here: 1150 us
  waiting for transfers between devices  656 us (57%)
  Pallas kernels  235 us (20%)
  other arithmetic  81.4 us (7%)
  starting transfers between devices  76.7 us (7%)
  local copies, waits for them, and re-layouts  72.5 us (6%)
  between operations  15.4 us (1%)
    ppermute x50, waiting for transfers between devices, send(): return lax.ppermute(value, 'bx', self.perm)  590 us
    pallas_call x6, Pallas kernels, up_call(): pl.pallas_call(functools.partial(up_kernel, head_dim), out_shape=(jax.Sha...  164 us
    pallas_call x6, Pallas kernels, down_call(): pl.pallas_call(down_kernel, out_shape=(shape, shape), in_specs=[smem, vme...  71.1 us
    ppermute x50, starting transfers between devices, send(): return lax.ppermute(value, 'bx', self.perm)  47.5 us
    ppermute x26, waiting for transfers between devices, swap_core(): return lax.ppermute(value, 'bx', core_perm)  33.5 us
    reduce_scatter x6, waiting for transfers between devices, device_program(): reduced = lax.psum_scatter(ordered, 'm', scatter_dimension=0)  31.9 us
    convert_element_type x6, other arithmetic, device_program(): (keep.astype(jnp.float32) + from_core.astype(jnp.float32)).astype(jnp.bfl...  29.4 us
    squeeze x10, local copies, waits for them, and re-layouts, take(): return lax.dynamic_slice(w, starts, [1] + sizes + list(tail))[0]  28.1 us
  transfers between devices with their start and end apart: 88, of which 34 were waited for; matrix products, arithmetic and copies ran while one was open for 12% of the time, Pallas kernels for 20%

profile of v1, /device:TPU:97, one launch (start us, length us, event | category | flops | bytes accessed | tf_op | source)
XLA Modules:
  0.0 1149.0 jit_solution(6435861030208793072)
XLA Ops:
  8.6 3.8 collective-permute-start.2
  12.4 8.3 collective-permute-done.2
  23.4 3.0 collective-permute-start.16
  26.4 3.4 dynamic-slice_bitcast_fusion.7
  31.5 2.7 collective-permute-start.60
  34.2 4.2 dynamic-slice_bitcast_fusion.2
  38.4 4.5 dynamic-slice_bitcast_fusion.1
  47.7 2.9 dynamic-slice_bitcast_fusion.24
  50.6 3.8 dynamic-slice_bitcast_fusion
  55.0 2.9 dynamic-slice_bitcast_fusion.22
  58.8 6.0 collective-permute-done.30
  82.6 30.5 %collective-permute-done.68 = bf16[128,1536]{1,0:T(8,128)(2,1)S(1)} collective-permute-done((bf16[128,1536]{1,0:T(8,128)(2,1)S(1)}, bf16[128,1536]{1,0:T(8,128)(2,1)S(1)}, u32[]{:S(2)}, u32[]{:S(2)}) %collective-permute-start.68) | collective-permute-done | bytes 393248 | tf_op jit(solution)/shard_map/ppermute | solution.py:202
  121.8 11.4 all-gather.7
  135.0 5.9 collective-permute-done.25.refs_5_
  140.8 3.3 collective-permute-start.3
  147.8 26.9 %collective-permute-done.9.refs_5_ = bf16[1536,512]{1,0:T(8,128)(2,1)} collective-permute-done((bf16[1536,512]{1,0:T(8,128)(2,1)}, bf16[1536,512]{1,0:T(8,128)(2,1)}, u32[]{:S(2)}, u32[]{:S(2)}) %collective-permute-start.9) | collective-permute-done | bytes 1572896 | tf_op jit(solution)/shard_map/ppermute | solution.py:202
  175.6 32.7 %collective-permute-done.5.refs_1_ = bf16[1536,512]{1,0:T(8,128)(2,1)} collective-permute-done((bf16[1536,512]{1,0:T(8,128)(2,1)}, bf16[1536,512]{1,0:T(8,128)(2,1)}, u32[]{:S(2)}, u32[]{:S(2)}) %collective-permute-start.5) | collective-permute-done | bytes 1572896 | tf_op jit(solution)/shard_map/ppermute | solution.py:202
  218.1 23.9 %collective-permute-done.21.refs_1_ = bf16[512,1536]{1,0:T(8,128)(2,1)} collective-permute-done((bf16[512,1536]{1,0:T(8,128)(2,1)}, bf16[512,1536]{1,0:T(8,128)(2,1)}, u32[]{:S(2)}, u32[]{:S(2)}) %collective-permute-start.21) | collective-permute-done | bytes 1572896 | tf_op jit(solution)/shard_map/ppermute | solution.py:202
  245.3 21.3 %collective-permute-done.11.refs_7_ = bf16[1536,512]{1,0:T(8,128)(2,1)} collective-permute-done((bf16[1536,512]{1,0:T(8,128)(2,1)}, bf16[1536,512]{1,0:T(8,128)(2,1)}, u32[]{:S(2)}, u32[]{:S(2)}) %collective-permute-start.11) | collective-permute-done | bytes 1572896 | tf_op jit(solution)/shard_map/ppermute | solution.py:202
  266.9 33.4 %collective-permute-done.7.refs_3_ = bf16[1536,512]{1,0:T(8,128)(2,1)} collective-permute-done((bf16[1536,512]{1,0:T(8,128)(2,1)}, bf16[1536,512]{1,0:T(8,128)(2,1)}, u32[]{:S(2)}, u32[]{:S(2)}) %collective-permute-start.7) | collective-permute-done | bytes 1572896 | tf_op jit(solution)/shard_map/ppermute | solution.py:202
  302.3 27.0 %shard_map.121 = (bf16[512,896]{1,0:T(8,128)(2,1)}, bf16[128,128]{1,0:T(8,128)(2,1)}, bf16[128,128]{1,0:T(8,128)(2,1)}) custom-call(s32[8]{0:T(128)} %convert_element_type.168.order_ref, s32[4]{0:T(128)} %reshape_squeeze.18.lens_ref, bf16[4,256,1536]{2,1,0:T(8,128)(2,1)} %bitcast.254, bf16[4,256,1536]{2,1,0:T(8,128)(2,1)} %collective-permute-done.3.other_ref, ...), custom_call_target="tpu_custom_call" | custom-call | flops 10468982784 | bytes 26738688 | tf_op jit(solution)/shard_map/pallas_call | solution.py:155
  329.3 63.6 %collective-permute-done.26.refs_6_ = bf16[384,1536]{1,0:T(8,128)(2,1)S(1)} collective-permute-done((bf16[384,1536]{1,0:T(8,128)(2,1)S(1)}, bf16[384,1536]{1,0:T(8,128)(2,1)S(1)}, u32[]{:S(2)}, u32[]{:S(2)}) %collective-permute-start.26) | collective-permute-done | bytes 1179680 | tf_op jit(solution)/shard_map/ppermute | solution.py:202
  392.9 25.4 %collective-permute-done.27.refs_7_ = bf16[384,1536]{1,0:T(8,128)(2,1)} collective-permute-done((bf16[384,1536]{1,0:T(8,128)(2,1)S(1)}, bf16[384,1536]{1,0:T(8,128)(2,1)}, u32[]{:S(2)}, u32[]{:S(2)}) %collective-permute-start.27) | collective-permute-done | bytes 1179680 | tf_op jit(solution)/shard_map/ppermute | solution.py:202
  419.5 11.8 %shard_map.122 = (bf16[4,256,1536]{2,1,0:T(8,128)(2,1)}, bf16[4,256,1536]{2,1,0:T(8,128)(2,1)}) custom-call(s32[8]{0:T(128)S(1)} %copy-done, bf16[512,896]{1,0:T(8,128)(2,1)S(1)} %copy-done.8, bf16[512,1536]{1,0:T(8,128)(2,1)} %pad_maximum_fusion.7.refs_0_, bf16[512,1536]{1,0:T(8,128)(2,1)} %collective-permute-done.21.refs_1_, ...), custom_call_target="tpu_custom_call" | custom-call | flops 5637144576 | bytes 17301504 | tf_op jit(solution)/shard_map/pallas_call | solution.py:181
  431.3 4.3 collective-permute-start.28
  435.7 5.5 collective-permute-done.28
  441.2 5.4 add_convert_fusion.5
  447.6 27.6 %shard_map.125 = (bf16[512,896]{1,0:T(8,128)(2,1)}, bf16[128,128]{1,0:T(8,128)(2,1)}, bf16[128,128]{1,0:T(8,128)(2,1)}) custom-call(s32[8]{0:T(128)} %convert_element_type.168.order_ref, s32[4]{0:T(128)} %reshape_squeeze.20.lens_ref, bf16[4,256,1536]{2,1,0:T(8,128)(2,1)} %bitcast.258, bf16[4,256,1536]{2,1,0:T(8,128)(2,1)} %collective-permute-done.61.other_ref, ...), custom_call_target="tpu_custom_call" | custom-call | flops 10468982784 | bytes 26738688 | tf_op jit(solution)/shard_map/pallas_call | solution.py:155
  476.4 11.9 %shard_map.126 = (bf16[4,256,1536]{2,1,0:T(8,128)(2,1)}, bf16[4,256,1536]{2,1,0:T(8,128)(2,1)}) custom-call(s32[8]{0:T(128)S(1)} %copy-done.1, bf16[512,896]{1,0:T(8,128)(2,1)S(1)} %copy-done.10, bf16[512,1536]{1,0:T(8,128)(2,1)} %pad_maximum_fusion.7.refs_0_, bf16[512,1536]{1,0:T(8,128)(2,1)} %collective-permute-done.21.refs_1_, ...), custom_call_target="tpu_custom_call" | custom-call | flops 5637144576 | bytes 17301504 | tf_op jit(solution)/shard_map/pallas_call | solution.py:181
  488.7 5.5 collective-permute-done.62
  494.2 4.5 add_convert_fusion.3
  500.8 11.5 %collective-permute-done.29 = bf16[128,1536]{1,0:T(8,128)(2,1)S(1)} collective-permute-done((bf16[128,1536]{1,0:T(8,128)(2,1)S(1)}, bf16[128,1536]{1,0:T(8,128)(2,1)S(1)}, u32[]{:S(2)}, u32[]{:S(2)}) %collective-permute-start.29) | collective-permute-done | bytes 393248 | tf_op jit(solution)/shard_map/ppermute | solution.py:202
  514.9 9.5 collective-permute-done.32
  527.0 27.3 %shard_map.129 = (bf16[512,896]{1,0:T(8,128)(2,1)}, bf16[128,128]{1,0:T(8,128)(2,1)}, bf16[128,128]{1,0:T(8,128)(2,1)}) custom-call(s32[8]{0:T(128)} %convert_element_type.168.order_ref, s32[4]{0:T(128)} %reshape_squeeze.22.lens_ref, bf16[4,256,1536]{2,1,0:T(8,128)(2,1)} %bitcast.262, bf16[4,256,1536]{2,1,0:T(8,128)(2,1)} %collective-permute-done.69.other_ref, ...), custom_call_target="tpu_custom_call" | custom-call | flops 10468982784 | bytes 26738688 | tf_op jit(solution)/shard_map/pallas_call | solution.py:155
  555.5 11.9 %shard_map.130 = (bf16[4,256,1536]{2,1,0:T(8,128)(2,1)}, bf16[4,256,1536]{2,1,0:T(8,128)(2,1)}) custom-call(s32[8]{0:T(128)S(1)} %copy-done.2, bf16[512,896]{1,0:T(8,128)(2,1)S(1)} %copy-done.7, bf16[512,1536]{1,0:T(8,128)(2,1)} %pad_maximum_fusion.7.refs_0_, bf16[512,1536]{1,0:T(8,128)(2,1)} %collective-permute-done.21.refs_1_, ...), custom_call_target="tpu_custom_call" | custom-call | flops 5637144576 | bytes 17301504 | tf_op jit(solution)/shard_map/pallas_call | solution.py:181
  569.2 5.5 collective-permute-done.70
  574.7 4.4 add_convert_fusion.1
  581.4 10.1 collective-permute-done.46
  593.7 8.9 collective-permute-done.48
  613.2 7.2 collective-permute-done.63
  623.8 3.4 constant_dynamic-slice_fusion.6
  627.2 18.9 %collective-permute-done.64 = bf16[128,1536]{1,0:T(8,128)(2,1)S(1)} collective-permute-done((bf16[128,1536]{1,0:T(8,128)(2,1)S(1)}, bf16[128,1536]{1,0:T(8,128)(2,1)S(1)}, u32[]{:S(2)}, u32[]{:S(2)}) %collective-permute-start.64) | collective-permute-done | bytes 393248 | tf_op jit(solution)/shard_map/ppermute | solution.py:202
  661.7 17.6 %collective-permute-done.55.refs_5_ = bf16[384,1536]{1,0:T(8,128)(2,1)S(1)} collective-permute-done((bf16[384,1536]{1,0:T(8,128)(2,1)S(1)}, bf16[384,1536]{1,0:T(8,128)(2,1)S(1)}, u32[]{:S(2)}, u32[]{:S(2)}) %collective-permute-start.55) | collective-permute-done | bytes 1179680 | tf_op jit(solution)/shard_map/ppermute | solution.py:202
  682.3 30.7 %collective-permute-done.35.refs_1_ = bf16[1536,512]{1,0:T(8,128)(2,1)} collective-permute-done((bf16[1536,512]{1,0:T(8,128)(2,1)}, bf16[1536,512]{1,0:T(8,128)(2,1)}, u32[]{:S(2)}, u32[]{:S(2)}) %collective-permute-start.35) | collective-permute-done | bytes 1572896 | tf_op jit(solution)/shard_map/ppermute | solution.py:202
  717.7 29.0 %collective-permute-done.39.refs_5_ = bf16[1536,512]{1,0:T(8,128)(2,1)} collective-permute-done((bf16[1536,512]{1,0:T(8,128)(2,1)}, bf16[1536,512]{1,0:T(8,128)(2,1)}, u32[]{:S(2)}, u32[]{:S(2)}) %collective-permute-start.39) | collective-permute-done | bytes 1572896 | tf_op jit(solution)/shard_map/ppermute | solution.py:202
  760.8 21.4 %collective-permute-done.51.refs_1_ = bf16[512,1536]{1,0:T(8,128)(2,1)} collective-permute-done((bf16[512,1536]{1,0:T(8,128)(2,1)}, bf16[512,1536]{1,0:T(8,128)(2,1)}, u32[]{:S(2)}, u32[]{:S(2)}) %collective-permute-start.51) | collective-permute-done | bytes 1572896 | tf_op jit(solution)/shard_map/ppermute | solution.py:202
  784.4 23.9 %collective-permute-done.45.refs_11_ = bf16[3,1536,128]{2,1,0:T(8,128)(2,1)S(1)} collective-permute-done((bf16[3,1536,128]{2,1,0:T(8,128)(2,1)}, bf16[3,1536,128]{2,1,0:T(8,128)(2,1)S(1)}, u32[]{:S(2)}, u32[]{:S(2)}) %collective-permute-start.45) | collective-permute-done | bytes 1179680 | tf_op jit(solution)/shard_map/ppermute | solution.py:202
  812.2 29.7 %collective-permute-done.41.refs_7_ = bf16[1536,512]{1,0:T(8,128)(2,1)S(1)} collective-permute-done((bf16[1536,512]{1,0:T(8,128)(2,1)}, bf16[1536,512]{1,0:T(8,128)(2,1)S(1)}, u32[]{:S(2)}, u32[]{:S(2)}) %collective-permute-start.41) | collective-permute-done | bytes 1572896 | tf_op jit(solution)/shard_map/ppermute | solution.py:202
  846.7 27.1 %shard_map.123 = (bf16[512,896]{1,0:T(8,128)(2,1)}, bf16[128,128]{1,0:T(8,128)(2,1)}, bf16[128,128]{1,0:T(8,128)(2,1)}) custom-call(s32[8]{0:T(128)} %convert_element_type.178.order_ref, s32[4]{0:T(128)} %reshape_squeeze.19.lens_ref, bf16[4,256,1536]{2,1,0:T(8,128)(2,1)} %bitcast.256, bf16[4,256,1536]{2,1,0:T(8,128)(2,1)} %collective-permute-done.33.other_ref, ...), custom_call_target="tpu_custom_call" | custom-call | flops 10468982784 | bytes 26738688 | tf_op jit(solution)/shard_map/pallas_call | solution.py:155
  873.7 60.9 %collective-permute-done.56.refs_6_ = bf16[384,1536]{1,0:T(8,128)(2,1)S(1)} collective-permute-done((bf16[384,1536]{1,0:T(8,128)(2,1)S(1)}, bf16[384,1536]{1,0:T(8,128)(2,1)S(1)}, u32[]{:S(2)}, u32[]{:S(2)}) %collective-permute-start.56) | collective-permute-done | bytes 1179680 | tf_op jit(solution)/shard_map/ppermute | solution.py:202
  934.7 25.4 %collective-permute-done.57.refs_7_ = bf16[384,1536]{1,0:T(8,128)(2,1)} collective-permute-done((bf16[384,1536]{1,0:T(8,128)(2,1)S(1)}, bf16[384,1536]{1,0:T(8,128)(2,1)}, u32[]{:S(2)}, u32[]{:S(2)}) %collective-permute-start.57) | collective-permute-done | bytes 1179680 | tf_op jit(solution)/shard_map/ppermute | solution.py:202
  961.2 11.8 %shard_map.124 = (bf16[4,256,1536]{2,1,0:T(8,128)(2,1)}, bf16[4,256,1536]{2,1,0:T(8,128)(2,1)}) custom-call(s32[8]{0:T(128)S(1)} %copy-done.3, bf16[512,896]{1,0:T(8,128)(2,1)S(1)} %copy-done.9, bf16[512,1536]{1,0:T(8,128)(2,1)} %pad_maximum_fusion.14.refs_0_, bf16[512,1536]{1,0:T(8,128)(2,1)} %collective-permute-done.51.refs_1_, ...), custom_call_target="tpu_custom_call" | custom-call | flops 5637144576 | bytes 17301504 | tf_op jit(solution)/shard_map/pallas_call | solution.py:181
  975.3 5.5 collective-permute-done.58
  980.8 5.4 add_convert_fusion.4
  987.3 27.6 %shard_map.127 = (bf16[512,896]{1,0:T(8,128)(2,1)}, bf16[128,128]{1,0:T(8,128)(2,1)}, bf16[128,128]{1,0:T(8,128)(2,1)}) custom-call(s32[8]{0:T(128)} %convert_element_type.178.order_ref, s32[4]{0:T(128)} %reshape_squeeze.21.lens_ref, bf16[4,256,1536]{2,1,0:T(8,128)(2,1)} %bitcast.260, bf16[4,256,1536]{2,1,0:T(8,128)(2,1)} %collective-permute-done.65.other_ref, ...), custom_call_target="tpu_custom_call" | custom-call | flops 10468982784 | bytes 26738688 | tf_op jit(solution)/shard_map/pallas_call | solution.py:155
  1016.1 11.9 %shard_map.128 = (bf16[4,256,1536]{2,1,0:T(8,128)(2,1)}, bf16[4,256,1536]{2,1,0:T(8,128)(2,1)}) custom-call(s32[8]{0:T(128)S(1)} %copy-done.4, bf16[512,896]{1,0:T(8,128)(2,1)S(1)} %copy-done.11, bf16[512,1536]{1,0:T(8,128)(2,1)} %pad_maximum_fusion.14.refs_0_, bf16[512,1536]{1,0:T(8,128)(2,1)} %collective-permute-done.51.refs_1_, ...), custom_call_target="tpu_custom_call" | custom-call | flops 5637144576 | bytes 17301504 | tf_op jit(solution)/shard_map/pallas_call | solution.py:181
  1028.6 5.5 collective-permute-done.66
  1034.1 5.4 add_convert_fusion.2
  1040.5 27.6 %shard_map.131 = (bf16[512,896]{1,0:T(8,128)(2,1)}, bf16[128,128]{1,0:T(8,128)(2,1)}, bf16[128,128]{1,0:T(8,128)(2,1)}) custom-call(s32[8]{0:T(128)} %convert_element_type.178.order_ref, s32[4]{0:T(128)} %reshape_squeeze.23.lens_ref, bf16[4,256,1536]{2,1,0:T(8,128)(2,1)} %bitcast.264, bf16[4,256,1536]{2,1,0:T(8,128)(2,1)} %collective-permute-done.73.other_ref, ...), custom_call_target="tpu_custom_call" | custom-call | flops 10468982784 | bytes 26738688 | tf_op jit(solution)/shard_map/pallas_call | solution.py:155
  1069.3 11.8 %shard_map.132 = (bf16[4,256,1536]{2,1,0:T(8,128)(2,1)}, bf16[4,256,1536]{2,1,0:T(8,128)(2,1)}) custom-call(s32[8]{0:T(128)S(1)} %copy-done.5, bf16[512,896]{1,0:T(8,128)(2,1)S(1)} %copy-done.6, bf16[512,1536]{1,0:T(8,128)(2,1)} %pad_maximum_fusion.14.refs_0_, bf16[512,1536]{1,0:T(8,128)(2,1)} %collective-permute-done.51.refs_1_, ...), custom_call_target="tpu_custom_call" | custom-call | flops 5637144576 | bytes 17301504 | tf_op jit(solution)/shard_map/pallas_call | solution.py:181
  1081.6 5.5 collective-permute-done.74
  1087.1 4.4 add_convert_fusion
  1097.7 31.9 %reduce-scatter.17.cloned.1.call-done = bf16[1,256,1536]{2,1,0:T(8,128)(2,1)} async-done(((bf16[4,256,1536]{2,1,0:T(8,128)(2,1)}), bf16[1,256,1536]{2,1,0:T(8,128)(2,1)}) %reduce-scatter.17.cloned.1.call-update) | async-done | bytes 786448 | tf_op jit(solution)/shard_map/reduce_scatter | solution.py:291
  1133.3 7.4 collective-permute-done.75
  (414 shorter events, 160.4 us)
Async XLA Ops:
  7.2 133.7 %all-gather.15.cloned.1.call-start = ((), (), s32[]{:S(2)}) async-start(), calls=%async_computation.12 | async-start | bytes 3932160 | tf_op jit(solution)/shard_map/all_gather | solution.py:283
  21.7 413.9 %all-gather.19.cloned.1.call-start = ((), (), s32[]{:S(2)}) async-start(), calls=%async_computation.14 | async-start | bytes 3932160 | tf_op jit(solution)/shard_map/all_gather | solution.py:283
  23.4 31.0 %collective-permute-start.16 = (bf16[768,256]{1,0:T(8,128)(2,1)}, bf16[768,256]{1,0:T(8,128)(2,1)}, u32[]{:S(2)}, u32[]{:S(2)}) collective-permute-start(bf16[768,256]{1,0:T(8,128)(2,1)} %get-tuple-element.137), channel_id=1, source_target_pairs={{0,6},{1,7},{2,4},{3,5},{4,2},{5,3},{6,0},{7,1},{8,14},{9,15},{10,... | collective-permute-start | bytes 1179656 | tf_op jit(solution)/shard_map/ppermute | solution.py:202
  26.4 39.9 %collective-permute-start.17 = (bf16[768,256]{1,0:T(8,128)(2,1)}, bf16[768,256]{1,0:T(8,128)(2,1)}, u32[]{:S(2)}, u32[]{:S(2)}) collective-permute-start(bf16[768,256]{1,0:T(8,128)(2,1)} %get-tuple-element.137), channel_id=1, source_target_pairs={{0,2},{1,3},{2,0},{3,1},{4,6},{5,7},{6,4},{7,5},{8,10},{9,11},{10,... | collective-permute-start | bytes 1179656 | tf_op jit(solution)/shard_map/ppermute | solution.py:202
  29.8 41.3 %collective-permute-start.12 = (bf16[6,768,128]{2,1,0:T(8,128)(2,1)}, bf16[6,768,128]{2,1,0:T(8,128)(2,1)}, u32[]{:S(2)}, u32[]{:S(2)}) collective-permute-start(bf16[6,768,128]{2,1,0:T(8,128)(2,1)} %get-tuple-element.98), channel_id=1, source_target_pairs={{0,1},{1,0},{2,3},{3,2},{4,5},{5,4},{6,7},{7,6},{8,9},{9,8},{10,11... | collective-permute-start | bytes 3538952 | tf_op jit(solution)/shard_map/ppermute | solution.py:215
  31.5 26.4 %collective-permute-start = (s32[3]{0:T(128)S(1)}, s32[3]{0:T(128)S(1)}, u32[]{:S(2)}, u32[]{:S(2)}) collective-permute-start(s32[3]{0:T(128)S(1)} %copy-done.73), channel_id=1, source_target_pairs={{0,6},{1,7},{2,4},{3,5},{4,2},{5,3},{6,0},{7,1},{8,14},{9,15},{10,... | collective-permute-start | bytes 44 | tf_op jit(solution)/shard_map/ppermute | solution.py:202
  31.5 34.8 %collective-permute-start.60 = (bf16[128,1536]{1,0:T(8,128)(2,1)S(1)}, bf16[128,1536]{1,0:T(8,128)(2,1)}, u32[]{:S(2)}, u32[]{:S(2)}) collective-permute-start(bf16[128,1536]{1,0:T(8,128)(2,1)S(1)} %get-tuple-element.121), channel_id=1, source_target_pairs={{0,6},{1,7},{2,4},{3,5},{4,2},{5,3},{6,0},{7,1},{8,14},{9,15},{10,... | collective-permute-start | bytes 1179656 | tf_op jit(solution)/shard_map/ppermute | solution.py:202
  54.4 15.1 %collective-permute-start.18 = (bf16[768,256]{1,0:T(8,128)(2,1)}, bf16[768,256]{1,0:T(8,128)(2,1)S(1)}, u32[]{:S(2)}, u32[]{:S(2)}) collective-permute-start(bf16[768,256]{1,0:T(8,128)(2,1)} %collective-permute-done.16), channel_id=1, source_target_pairs={{0,2},{1,3},{2,0},{3,1},{4,6},{5,7},{6,4},{7,5},{8,10},{9,11},{10,... | collective-permute-start | bytes 1179656 | tf_op jit(solution)/shard_map/ppermute | solution.py:202
  68.7 430.1 %all-gather.23.cloned.1.call-start = ((), (), s32[]{:S(2)}) async-start(), calls=%async_computation.16 | async-start | bytes 3932160 | tf_op jit(solution)/shard_map/all_gather | solution.py:283
  69.5 43.9 %collective-permute-start.20 = (bf16[1024,768]{1,0:T(8,128)(2,1)}, bf16[1024,768]{1,0:T(8,128)(2,1)S(1)}, u32[]{:S(2)}, u32[]{:S(2)}) collective-permute-start(bf16[1024,768]{1,0:T(8,128)(2,1)} %get-tuple-element.74), channel_id=1, source_target_pairs={{0,1},{1,0},{2,3},{3,2},{4,5},{5,4},{6,7},{7,6},{8,9},{9,8},{10,11... | collective-permute-start | bytes 4718600 | tf_op jit(solution)/shard_map/ppermute | solution.py:215
  73.5 46.8 %collective-permute-start.19 = (bf16[4,768,256]{2,1,0:T(8,128)(2,1)S(1)}, bf16[4,768,256]{2,1,0:T(8,128)(2,1)S(1)}, u32[]{:S(2)}, u32[]{:S(2)}) collective-permute-start(bf16[4,768,256]{2,1,0:T(8,128)(2,1)S(1)} %pad_maximum_fusion.6), channel_id=1, source_target_pairs={{0,1},{1,0},{2,3},{3,2},{4,5},{5,4},{6,7},{7,6},{8,9},{9,8},{10,11... | collective-permute-start | bytes 4718600 | tf_op jit(solution)/shard_map/ppermute | solution.py:215
  76.1 42.4 %collective-permute-start.13 = (bf16[3,1536,128]{2,1,0:T(8,128)(2,1)S(1)}, bf16[3,1536,128]{2,1,0:T(8,128)(2,1)}, u32[]{:S(2)}, u32[]{:S(2)}) collective-permute-start(bf16[3,1536,128]{2,1,0:T(8,128)(2,1)S(1)} %pad_maximum_fusion.17), channel_id=1, source_target_pairs={{0,6},{1,7},{2,4},{3,5},{4,2},{5,3},{6,0},{7,1},{8,14},{9,15},{10,... | collective-permute-start | bytes 3538952 | tf_op jit(solution)/shard_map/ppermute | solution.py:202
  76.5 36.6 %collective-permute-start.68 = (bf16[128,1536]{1,0:T(8,128)(2,1)S(1)}, bf16[128,1536]{1,0:T(8,128)(2,1)S(1)}, u32[]{:S(2)}, u32[]{:S(2)}) collective-permute-start(bf16[128,1536]{1,0:T(8,128)(2,1)S(1)} %get-tuple-element.120), channel_id=1, source_target_pairs={{0,6},{1,7},{2,4},{3,5},{4,2},{5,3},{6,0},{7,1},{8,14},{9,15},{10,... | collective-permute-start | bytes 1179656 | tf_op jit(solution)/shard_map/ppermute | solution.py:202
  79.0 41.4 %collective-permute-start.14 = (bf16[3,1536,128]{2,1,0:T(8,128)(2,1)S(1)}, bf16[3,1536,128]{2,1,0:T(8,128)(2,1)S(1)}, u32[]{:S(2)}, u32[]{:S(2)}) collective-permute-start(bf16[3,1536,128]{2,1,0:T(8,128)(2,1)S(1)} %pad_maximum_fusion.16.refs_8_), channel_id=1, source_target_pairs={{0,2},{1,3},{2,0},{3,1},{4,6},{5,7},{6,4},{7,5},{8,10},{9,11},{10,... | collective-permute-start | bytes 3538952 | tf_op jit(solution)/shard_map/ppermute | solution.py:202
  113.1 27.7 %collective-permute-start.25 = (bf16[384,1536]{1,0:T(8,128)(2,1)S(1)}, bf16[384,1536]{1,0:T(8,128)(2,1)S(1)}, u32[]{:S(2)}, u32[]{:S(2)}) collective-permute-start(bf16[384,1536]{1,0:T(8,128)(2,1)S(1)} %pad_maximum_fusion.19), channel_id=1, source_target_pairs={{0,6},{1,7},{2,4},{3,5},{4,2},{5,3},{6,0},{7,1},{8,14},{9,15},{10,... | collective-permute-start | bytes 3538952 | tf_op jit(solution)/shard_map/ppermute | solution.py:202
  113.4 61.2 %collective-permute-start.9 = (bf16[1536,512]{1,0:T(8,128)(2,1)}, bf16[1536,512]{1,0:T(8,128)(2,1)}, u32[]{:S(2)}, u32[]{:S(2)}) collective-permute-start(bf16[1536,512]{1,0:T(8,128)(2,1)} %pad_maximum_fusion.5), channel_id=1, source_target_pairs={{0,6},{1,7},{2,4},{3,5},{4,2},{5,3},{6,0},{7,1},{8,14},{9,15},{10,... | collective-permute-start | bytes 4718600 | tf_op jit(solution)/shard_map/ppermute | solution.py:202
  118.5 89.9 %collective-permute-start.5 = (bf16[1536,512]{1,0:T(8,128)(2,1)}, bf16[1536,512]{1,0:T(8,128)(2,1)}, u32[]{:S(2)}, u32[]{:S(2)}) collective-permute-start(bf16[1536,512]{1,0:T(8,128)(2,1)} %pad_maximum_fusion.3), channel_id=1, source_target_pairs={{0,6},{1,7},{2,4},{3,5},{4,2},{5,3},{6,0},{7,1},{8,14},{9,15},{10,... | collective-permute-start | bytes 4718600 | tf_op jit(solution)/shard_map/ppermute | solution.py:202
  120.3 89.3 %collective-permute-start.10 = (bf16[1536,512]{1,0:T(8,128)(2,1)}, bf16[1536,512]{1,0:T(8,128)(2,1)}, u32[]{:S(2)}, u32[]{:S(2)}) collective-permute-start(bf16[1536,512]{1,0:T(8,128)(2,1)} %pad_maximum_fusion.4.refs_4_), channel_id=1, source_target_pairs={{0,2},{1,3},{2,0},{3,1},{4,6},{5,7},{6,4},{7,5},{8,10},{9,11},{10,... | collective-permute-start | bytes 4718600 | tf_op jit(solution)/shard_map/ppermute | solution.py:202
  120.4 90.7 %collective-permute-start.6 = (bf16[1536,512]{1,0:T(8,128)(2,1)}, bf16[1536,512]{1,0:T(8,128)(2,1)}, u32[]{:S(2)}, u32[]{:S(2)}) collective-permute-start(bf16[1536,512]{1,0:T(8,128)(2,1)} %pad_maximum_fusion.2.refs_0_), channel_id=1, source_target_pairs={{0,2},{1,3},{2,0},{3,1},{4,6},{5,7},{6,4},{7,5},{8,10},{9,11},{10,... | collective-permute-start | bytes 4718600 | tf_op jit(solution)/shard_map/ppermute | solution.py:202
  140.8 161.4 %collective-permute-start.3 = (bf16[4,256,1536]{2,1,0:T(8,128)(2,1)}, bf16[4,256,1536]{2,1,0:T(8,128)(2,1)}, u32[]{:S(2)}, u32[]{:S(2)}) collective-permute-start(bf16[4,256,1536]{2,1,0:T(8,128)(2,1)} %bitcast.253), channel_id=1, source_target_pairs={{0,1},{1,0},{2,3},{3,2},{4,5},{5,4},{6,7},{7,6},{8,9},{9,8},{10,11... | collective-permute-start | bytes 9437192 | tf_op jit(solution)/shard_map/ppermute | solution.py:215
  174.6 67.4 %collective-permute-start.21 = (bf16[512,1536]{1,0:T(8,128)(2,1)}, bf16[512,1536]{1,0:T(8,128)(2,1)}, u32[]{:S(2)}, u32[]{:S(2)}) collective-permute-start(bf16[512,1536]{1,0:T(8,128)(2,1)} %pad_maximum_fusion.8), channel_id=1, source_target_pairs={{0,6},{1,7},{2,4},{3,5},{4,2},{5,3},{6,0},{7,1},{8,14},{9,15},{10,... | collective-permute-start | bytes 4718600 | tf_op jit(solution)/shard_map/ppermute | solution.py:202
  208.4 33.7 %collective-permute-start.15 = (bf16[3,1536,128]{2,1,0:T(8,128)(2,1)}, bf16[3,1536,128]{2,1,0:T(8,128)(2,1)}, u32[]{:S(2)}, u32[]{:S(2)}) collective-permute-start(bf16[3,1536,128]{2,1,0:T(8,128)(2,1)} %collective-permute-done.13.refs_9_), channel_id=1, source_target_pairs={{0,2},{1,3},{2,0},{3,1},{4,6},{5,7},{6,4},{7,5},{8,10},{9,11},{10,... | collective-permute-start | bytes 3538952 | tf_op jit(solution)/shard_map/ppermute | solution.py:202
  209.6 57.0 %collective-permute-start.11 = (bf16[1536,512]{1,0:T(8,128)(2,1)}, bf16[1536,512]{1,0:T(8,128)(2,1)}, u32[]{:S(2)}, u32[]{:S(2)}) collective-permute-start(bf16[1536,512]{1,0:T(8,128)(2,1)} %collective-permute-done.9.refs_5_), channel_id=1, source_target_pairs={{0,2},{1,3},{2,0},{3,1},{4,6},{5,7},{6,4},{7,5},{8,10},{9,11},{10,... | collective-permute-start | bytes 4718600 | tf_op jit(solution)/shard_map/ppermute | solution.py:202
  211.1 89.2 %collective-permute-start.7 = (bf16[1536,512]{1,0:T(8,128)(2,1)}, bf16[1536,512]{1,0:T(8,128)(2,1)}, u32[]{:S(2)}, u32[]{:S(2)}) collective-permute-start(bf16[1536,512]{1,0:T(8,128)(2,1)} %collective-permute-done.5.refs_1_), channel_id=1, source_target_pairs={{0,2},{1,3},{2,0},{3,1},{4,6},{5,7},{6,4},{7,5},{8,10},{9,11},{10,... | collective-permute-start | bytes 4718600 | tf_op jit(solution)/shard_map/ppermute | solution.py:202
  214.1 285.2 %reduce-scatter.7.cloned.1.call-start = ((), (), s32[]{:S(2)}) async-start(), calls=%async_computation.6 | async-start | bytes 3932160 | tf_op jit(solution)/shard_map/reduce_scatter | solution.py:291
  242.1 150.8 %collective-permute-start.22 = (bf16[512,1536]{1,0:T(8,128)(2,1)}, bf16[512,1536]{1,0:T(8,128)(2,1)}, u32[]{:S(2)}, u32[]{:S(2)}) collective-permute-start(bf16[512,1536]{1,0:T(8,128)(2,1)} %pad_maximum_fusion.7.refs_0_), channel_id=1, source_target_pairs={{0,2},{1,3},{2,0},{3,1},{4,6},{5,7},{6,4},{7,5},{8,10},{9,11},{10,... | collective-permute-start | bytes 4718600 | tf_op jit(solution)/shard_map/ppermute | solution.py:202
  242.1 176.2 %collective-permute-start.23 = (bf16[512,1536]{1,0:T(8,128)(2,1)}, bf16[512,1536]{1,0:T(8,128)(2,1)}, u32[]{:S(2)}, u32[]{:S(2)}) collective-permute-start(bf16[512,1536]{1,0:T(8,128)(2,1)} %collective-permute-done.21.refs_1_), channel_id=1, source_target_pairs={{0,2},{1,3},{2,0},{3,1},{4,6},{5,7},{6,4},{7,5},{8,10},{9,11},{10,... | collective-permute-start | bytes 4718600 | tf_op jit(solution)/shard_map/ppermute | solution.py:202
  266.6 126.3 %collective-permute-start.26 = (bf16[384,1536]{1,0:T(8,128)(2,1)S(1)}, bf16[384,1536]{1,0:T(8,128)(2,1)S(1)}, u32[]{:S(2)}, u32[]{:S(2)}) collective-permute-start(bf16[384,1536]{1,0:T(8,128)(2,1)S(1)} %pad_maximum_fusion.18.refs_4_), channel_id=1, source_target_pairs={{0,2},{1,3},{2,0},{3,1},{4,6},{5,7},{6,4},{7,5},{8,10},{9,11},{10,... | collective-permute-start | bytes 3538952 | tf_op jit(solution)/shard_map/ppermute | solution.py:202
  300.3 118.0 %collective-permute-start.27 = (bf16[384,1536]{1,0:T(8,128)(2,1)S(1)}, bf16[384,1536]{1,0:T(8,128)(2,1)}, u32[]{:S(2)}, u32[]{:S(2)}) collective-permute-start(bf16[384,1536]{1,0:T(8,128)(2,1)S(1)} %collective-permute-done.25.refs_5_), channel_id=1, source_target_pairs={{0,2},{1,3},{2,0},{3,1},{4,6},{5,7},{6,4},{7,5},{8,10},{9,11},{10,... | collective-permute-start | bytes 3538952 | tf_op jit(solution)/shard_map/ppermute | solution.py:202
  446.6 161.5 %reduce-scatter.11.cloned.1.call-start = ((), (), s32[]{:S(2)}) async-start(), calls=%async_computation.8 | async-start | bytes 3932160 | tf_op jit(solution)/shard_map/reduce_scatter | solution.py:291
  498.8 180.6 %all-gather.17.cloned.1.call-start = ((), (), s32[]{:S(2)}) async-start(), calls=%async_computation.13 | async-start | bytes 3932160 | tf_op jit(solution)/shard_map/all_gather | solution.py:283
  498.9 28.1 %collective-permute-start.69 = (bf16[4,256,1536]{2,1,0:T(8,128)(2,1)}, bf16[4,256,1536]{2,1,0:T(8,128)(2,1)}, u32[]{:S(2)}, u32[]{:S(2)}) collective-permute-start(bf16[4,256,1536]{2,1,0:T(8,128)(2,1)} %bitcast.261), channel_id=1, source_target_pairs={{0,1},{1,0},{2,3},{3,2},{4,5},{5,4},{6,7},{7,6},{8,9},{9,8},{10,11... | collective-permute-start | bytes 9437192 | tf_op jit(solution)/shard_map/ppermute | solution.py:215
  526.5 154.0 %reduce-scatter.15.cloned.1.call-start = ((), (), s32[]{:S(2)}) async-start(), calls=%async_computation.10 | async-start | bytes 3932160 | tf_op jit(solution)/shard_map/reduce_scatter | solution.py:291
  579.1 396.0 %all-gather.21.cloned.1.call-start = ((), (), s32[]{:S(2)}) async-start(), calls=%async_computation.15 | async-start | bytes 3932160 | tf_op jit(solution)/shard_map/all_gather | solution.py:283
  580.3 25.3 %collective-permute-start.42 = (bf16[6,768,128]{2,1,0:T(8,128)(2,1)S(1)}, bf16[6,768,128]{2,1,0:T(8,128)(2,1)}, u32[]{:S(2)}, u32[]{:S(2)}) collective-permute-start(bf16[6,768,128]{2,1,0:T(8,128)(2,1)S(1)} %copy-done.47), channel_id=1, source_target_pairs={{0,1},{1,0},{2,3},{3,2},{4,5},{5,4},{6,7},{7,6},{8,9},{9,8},{10,11... | collective-permute-start | bytes 3538952 | tf_op jit(solution)/shard_map/ppermute | solution.py:215
  591.9 29.9 %collective-permute-start.34 = (bf16[768,1024]{1,0:T(8,128)(2,1)}, bf16[768,1024]{1,0:T(8,128)(2,1)}, u32[]{:S(2)}, u32[]{:S(2)}) collective-permute-start(bf16[768,1024]{1,0:T(8,128)(2,1)} %get-tuple-element.85), channel_id=1, source_target_pairs={{0,1},{1,0},{2,3},{3,2},{4,5},{5,4},{6,7},{7,6},{8,9},{9,8},{10,11... | collective-permute-start | bytes 4718600 | tf_op jit(solution)/shard_map/ppermute | solution.py:215
  593.1 30.4 %collective-permute-start.38 = (bf16[768,1024]{1,0:T(8,128)(2,1)}, bf16[768,1024]{1,0:T(8,128)(2,1)}, u32[]{:S(2)}, u32[]{:S(2)}) collective-permute-start(bf16[768,1024]{1,0:T(8,128)(2,1)} %get-tuple-element.79), channel_id=1, source_target_pairs={{0,1},{1,0},{2,3},{3,2},{4,5},{5,4},{6,7},{7,6},{8,9},{9,8},{10,11... | collective-permute-start | bytes 4718600 | tf_op jit(solution)/shard_map/ppermute | solution.py:215
  593.1 58.6 %collective-permute-start.50 = (bf16[1024,768]{1,0:T(8,128)(2,1)}, bf16[1024,768]{1,0:T(8,128)(2,1)}, u32[]{:S(2)}, u32[]{:S(2)}) collective-permute-start(bf16[1024,768]{1,0:T(8,128)(2,1)} %get-tuple-element.73), channel_id=1, source_target_pairs={{0,1},{1,0},{2,3},{3,2},{4,5},{5,4},{6,7},{7,6},{8,9},{9,8},{10,11... | collective-permute-start | bytes 4718600 | tf_op jit(solution)/shard_map/ppermute | solution.py:215
  610.8 43.6 %collective-permute-start.43 = (bf16[3,1536,128]{2,1,0:T(8,128)(2,1)}, bf16[3,1536,128]{2,1,0:T(8,128)(2,1)}, u32[]{:S(2)}, u32[]{:S(2)}) collective-permute-start(bf16[3,1536,128]{2,1,0:T(8,128)(2,1)} %pad_maximum_fusion.21), channel_id=1, source_target_pairs={{0,2},{1,3},{2,0},{3,1},{4,6},{5,7},{6,4},{7,5},{8,10},{9,11},{10,... | collective-permute-start | bytes 3538952 | tf_op jit(solution)/shard_map/ppermute | solution.py:202
  620.6 25.6 %collective-permute-start.64 = (bf16[128,1536]{1,0:T(8,128)(2,1)S(1)}, bf16[128,1536]{1,0:T(8,128)(2,1)S(1)}, u32[]{:S(2)}, u32[]{:S(2)}) collective-permute-start(bf16[128,1536]{1,0:T(8,128)(2,1)S(1)} %fusion.7), channel_id=1, source_target_pairs={{0,2},{1,3},{2,0},{3,1},{4,6},{5,7},{6,4},{7,5},{8,10},{9,11},{10,... | collective-permute-start | bytes 1179656 | tf_op jit(solution)/shard_map/ppermute | solution.py:202
  621.8 38.1 %collective-permute-start.49 = (bf16[4,768,256]{2,1,0:T(8,128)(2,1)}, bf16[4,768,256]{2,1,0:T(8,128)(2,1)}, u32[]{:S(2)}, u32[]{:S(2)}) collective-permute-start(bf16[4,768,256]{2,1,0:T(8,128)(2,1)} %pad_maximum_fusion.13), channel_id=1, source_target_pairs={{0,1},{1,0},{2,3},{3,2},{4,5},{5,4},{6,7},{7,6},{8,9},{9,8},{10,11... | collective-permute-start | bytes 4718600 | tf_op jit(solution)/shard_map/ppermute | solution.py:215
  623.4 32.9 %collective-permute-start.44 = (bf16[3,1536,128]{2,1,0:T(8,128)(2,1)}, bf16[3,1536,128]{2,1,0:T(8,128)(2,1)}, u32[]{:S(2)}, u32[]{:S(2)}) collective-permute-start(bf16[3,1536,128]{2,1,0:T(8,128)(2,1)} %pad_maximum_fusion.20.refs_8_), channel_id=1, source_target_pairs={{0,6},{1,7},{2,4},{3,5},{4,2},{5,3},{6,0},{7,1},{8,14},{9,15},{10,... | collective-permute-start | bytes 3538952 | tf_op jit(solution)/shard_map/ppermute | solution.py:202
  649.0 379.5 %all-gather.25.cloned.1.call-start = ((), (), s32[]{:S(2)}) async-start(), calls=%async_computation.17 | async-start | bytes 3932160 | tf_op jit(solution)/shard_map/all_gather | solution.py:283
  651.7 27.6 %collective-permute-start.55 = (bf16[384,1536]{1,0:T(8,128)(2,1)S(1)}, bf16[384,1536]{1,0:T(8,128)(2,1)S(1)}, u32[]{:S(2)}, u32[]{:S(2)}) collective-permute-start(bf16[384,1536]{1,0:T(8,128)(2,1)S(1)} %copy-done.49), channel_id=1, source_target_pairs={{0,2},{1,3},{2,0},{3,1},{4,6},{5,7},{6,4},{7,5},{8,10},{9,11},{10,... | collective-permute-start | bytes 3538952 | tf_op jit(solution)/shard_map/ppermute | solution.py:202
  651.7 61.3 %collective-permute-start.35 = (bf16[1536,512]{1,0:T(8,128)(2,1)}, bf16[1536,512]{1,0:T(8,128)(2,1)}, u32[]{:S(2)}, u32[]{:S(2)}) collective-permute-start(bf16[1536,512]{1,0:T(8,128)(2,1)} %pad_maximum_fusion.10), channel_id=1, source_target_pairs={{0,2},{1,3},{2,0},{3,1},{4,6},{5,7},{6,4},{7,5},{8,10},{9,11},{10,... | collective-permute-start | bytes 4718600 | tf_op jit(solution)/shard_map/ppermute | solution.py:202
  654.4 92.3 %collective-permute-start.39 = (bf16[1536,512]{1,0:T(8,128)(2,1)}, bf16[1536,512]{1,0:T(8,128)(2,1)}, u32[]{:S(2)}, u32[]{:S(2)}) collective-permute-start(bf16[1536,512]{1,0:T(8,128)(2,1)} %pad_maximum_fusion.12), channel_id=1, source_target_pairs={{0,2},{1,3},{2,0},{3,1},{4,6},{5,7},{6,4},{7,5},{8,10},{9,11},{10,... | collective-permute-start | bytes 4718600 | tf_op jit(solution)/shard_map/ppermute | solution.py:202
  656.3 90.4 %collective-permute-start.36 = (bf16[1536,512]{1,0:T(8,128)(2,1)}, bf16[1536,512]{1,0:T(8,128)(2,1)}, u32[]{:S(2)}, u32[]{:S(2)}) collective-permute-start(bf16[1536,512]{1,0:T(8,128)(2,1)} %pad_maximum_fusion.9.refs_0_), channel_id=1, source_target_pairs={{0,6},{1,7},{2,4},{3,5},{4,2},{5,3},{6,0},{7,1},{8,14},{9,15},{10,... | collective-permute-start | bytes 4718600 | tf_op jit(solution)/shard_map/ppermute | solution.py:202
  659.9 92.6 %collective-permute-start.40 = (bf16[1536,512]{1,0:T(8,128)(2,1)}, bf16[1536,512]{1,0:T(8,128)(2,1)}, u32[]{:S(2)}, u32[]{:S(2)}) collective-permute-start(bf16[1536,512]{1,0:T(8,128)(2,1)} %pad_maximum_fusion.11.refs_4_), channel_id=1, source_target_pairs={{0,6},{1,7},{2,4},{3,5},{4,2},{5,3},{6,0},{7,1},{8,14},{9,15},{10,... | collective-permute-start | bytes 4718600 | tf_op jit(solution)/shard_map/ppermute | solution.py:202
  679.3 167.3 %collective-permute-start.33 = (bf16[4,256,1536]{2,1,0:T(8,128)(2,1)}, bf16[4,256,1536]{2,1,0:T(8,128)(2,1)}, u32[]{:S(2)}, u32[]{:S(2)}) collective-permute-start(bf16[4,256,1536]{2,1,0:T(8,128)(2,1)} %bitcast.255), channel_id=1, source_target_pairs={{0,1},{1,0},{2,3},{3,2},{4,5},{5,4},{6,7},{7,6},{8,9},{9,8},{10,11... | collective-permute-start | bytes 9437192 | tf_op jit(solution)/shard_map/ppermute | solution.py:215
  713.0 39.9 %collective-permute-start.71 = (bf16[128,1536]{1,0:T(8,128)(2,1)}, bf16[128,1536]{1,0:T(8,128)(2,1)}, u32[]{:S(2)}, u32[]{:S(2)}) collective-permute-start(bf16[128,1536]{1,0:T(8,128)(2,1)} %slice_bitcast_fusion.10), channel_id=1, source_target_pairs={{0,6},{1,7},{2,4},{3,5},{4,2},{5,3},{6,0},{7,1},{8,14},{9,15},{10,... | collective-permute-start | bytes 1179656 | tf_op jit(solution)/shard_map/ppermute | solution.py:202
  746.7 35.4 %collective-permute-start.51 = (bf16[512,1536]{1,0:T(8,128)(2,1)}, bf16[512,1536]{1,0:T(8,128)(2,1)}, u32[]{:S(2)}, u32[]{:S(2)}) collective-permute-start(bf16[512,1536]{1,0:T(8,128)(2,1)} %pad_maximum_fusion.15), channel_id=1, source_target_pairs={{0,2},{1,3},{2,0},{3,1},{4,6},{5,7},{6,4},{7,5},{8,10},{9,11},{10,... | collective-permute-start | bytes 4718600 | tf_op jit(solution)/shard_map/ppermute | solution.py:202
  746.7 63.8 %collective-permute-start.37 = (bf16[1536,512]{1,0:T(8,128)(2,1)}, bf16[1536,512]{1,0:T(8,128)(2,1)}, u32[]{:S(2)}, u32[]{:S(2)}) collective-permute-start(bf16[1536,512]{1,0:T(8,128)(2,1)} %collective-permute-done.35.refs_1_), channel_id=1, source_target_pairs={{0,6},{1,7},{2,4},{3,5},{4,2},{5,3},{6,0},{7,1},{8,14},{9,15},{10,... | collective-permute-start | bytes 4718600 | tf_op jit(solution)/shard_map/ppermute | solution.py:202
  752.4 55.8 %collective-permute-start.45 = (bf16[3,1536,128]{2,1,0:T(8,128)(2,1)}, bf16[3,1536,128]{2,1,0:T(8,128)(2,1)S(1)}, u32[]{:S(2)}, u32[]{:S(2)}) collective-permute-start(bf16[3,1536,128]{2,1,0:T(8,128)(2,1)} %collective-permute-done.43.refs_9_), channel_id=1, source_target_pairs={{0,6},{1,7},{2,4},{3,5},{4,2},{5,3},{6,0},{7,1},{8,14},{9,15},{10,... | collective-permute-start | bytes 3538952 | tf_op jit(solution)/shard_map/ppermute | solution.py:202
  753.0 89.0 %collective-permute-start.41 = (bf16[1536,512]{1,0:T(8,128)(2,1)}, bf16[1536,512]{1,0:T(8,128)(2,1)S(1)}, u32[]{:S(2)}, u32[]{:S(2)}) collective-permute-start(bf16[1536,512]{1,0:T(8,128)(2,1)} %collective-permute-done.39.refs_5_), channel_id=1, source_target_pairs={{0,6},{1,7},{2,4},{3,5},{4,2},{5,3},{6,0},{7,1},{8,14},{9,15},{10,... | collective-permute-start | bytes 4718600 | tf_op jit(solution)/shard_map/ppermute | solution.py:202
  782.1 152.5 %collective-permute-start.52 = (bf16[512,1536]{1,0:T(8,128)(2,1)}, bf16[512,1536]{1,0:T(8,128)(2,1)}, u32[]{:S(2)}, u32[]{:S(2)}) collective-permute-start(bf16[512,1536]{1,0:T(8,128)(2,1)} %pad_maximum_fusion.14.refs_0_), channel_id=1, source_target_pairs={{0,6},{1,7},{2,4},{3,5},{4,2},{5,3},{6,0},{7,1},{8,14},{9,15},{10,... | collective-permute-start | bytes 4718600 | tf_op jit(solution)/shard_map/ppermute | solution.py:202
  808.3 151.8 %collective-permute-start.53 = (bf16[512,1536]{1,0:T(8,128)(2,1)}, bf16[512,1536]{1,0:T(8,128)(2,1)}, u32[]{:S(2)}, u32[]{:S(2)}) collective-permute-start(bf16[512,1536]{1,0:T(8,128)(2,1)} %collective-permute-done.51.refs_1_), channel_id=1, source_target_pairs={{0,6},{1,7},{2,4},{3,5},{4,2},{5,3},{6,0},{7,1},{8,14},{9,15},{10,... | collective-permute-start | bytes 4718600 | tf_op jit(solution)/shard_map/ppermute | solution.py:202
  810.5 33.7 %collective-permute-start.72 = (bf16[128,1536]{1,0:T(8,128)(2,1)S(1)}, bf16[128,1536]{1,0:T(8,128)(2,1)S(1)}, u32[]{:S(2)}, u32[]{:S(2)}) collective-permute-start(bf16[128,1536]{1,0:T(8,128)(2,1)S(1)} %fusion.3), channel_id=1, source_target_pairs={{0,2},{1,3},{2,0},{3,1},{4,6},{5,7},{6,4},{7,5},{8,10},{9,11},{10,... | collective-permute-start | bytes 1179656 | tf_op jit(solution)/shard_map/ppermute | solution.py:202
  842.0 92.7 %collective-permute-start.56 = (bf16[384,1536]{1,0:T(8,128)(2,1)S(1)}, bf16[384,1536]{1,0:T(8,128)(2,1)S(1)}, u32[]{:S(2)}, u32[]{:S(2)}) collective-permute-start(bf16[384,1536]{1,0:T(8,128)(2,1)S(1)} %pad_maximum_fusion.22.refs_4_), channel_id=1, source_target_pairs={{0,6},{1,7},{2,4},{3,5},{4,2},{5,3},{6,0},{7,1},{8,14},{9,15},{10,... | collective-permute-start | bytes 3538952 | tf_op jit(solution)/shard_map/ppermute | solution.py:202
  844.2 115.8 %collective-permute-start.57 = (bf16[384,1536]{1,0:T(8,128)(2,1)S(1)}, bf16[384,1536]{1,0:T(8,128)(2,1)}, u32[]{:S(2)}, u32[]{:S(2)}) collective-permute-start(bf16[384,1536]{1,0:T(8,128)(2,1)S(1)} %collective-permute-done.55.refs_5_), channel_id=1, source_target_pairs={{0,6},{1,7},{2,4},{3,5},{4,2},{5,3},{6,0},{7,1},{8,14},{9,15},{10,... | collective-permute-start | bytes 3538952 | tf_op jit(solution)/shard_map/ppermute | solution.py:202
  846.4 247.5 %reduce-scatter.9.cloned.1.call-start = ((), (), s32[]{:S(2)}) async-start(), calls=%async_computation.7 | async-start | bytes 3932160 | tf_op jit(solution)/shard_map/reduce_scatter | solution.py:291
  986.2 109.3 %reduce-scatter.13.cloned.1.call-start = ((), (), s32[]{:S(2)}) async-start(), calls=%async_computation.9 | async-start | bytes 3932160 | tf_op jit(solution)/shard_map/reduce_scatter | solution.py:291
  1039.6 90.0 %reduce-scatter.17.cloned.1.call-start = ((), (), s32[]{:S(2)}) async-start(), calls=%async_computation.11 | async-start | bytes 3932160 | tf_op jit(solution)/shard_map/reduce_scatter | solution.py:291
  1095.0 37.0 %collective-permute-start.59 = (bf16[128,1536]{1,0:T(8,128)(2,1)S(1)}, bf16[128,1536]{1,0:T(8,128)(2,1)S(1)}, u32[]{:S(2)}, u32[]{:S(2)}) collective-permute-start(bf16[128,1536]{1,0:T(8,128)(2,1)S(1)} %slice_bitcast_fusion.16), channel_id=1, source_target_pairs={{0,2},{1,3},{2,0},{3,1},{4,6},{5,7},{6,4},{7,5},{8,10},{9,11},{10,... | collective-permute-start | bytes 1179656 | tf_op jit(solution)/shard_map/ppermute | solution.py:202
  1096.6 36.5 %collective-permute-start.67 = (bf16[128,1536]{1,0:T(8,128)(2,1)S(1)}, bf16[128,1536]{1,0:T(8,128)(2,1)S(1)}, u32[]{:S(2)}, u32[]{:S(2)}) collective-permute-start(bf16[128,1536]{1,0:T(8,128)(2,1)S(1)} %slice_bitcast_fusion.12), channel_id=1, source_target_pairs={{0,2},{1,3},{2,0},{3,1},{4,6},{5,7},{6,4},{7,5},{8,10},{9,11},{10,... | collective-permute-start | bytes 1179656 | tf_op jit(solution)/shard_map/ppermute | solution.py:202
  (111 other events, 1579.1 us)
Sparse Core Ops, SparseCore 0:
  21.8 40.7 all-gather.14
  68.9 37.3 all-gather.18
  214.2 41.7 all-gather.22
  446.8 35.8 reduce-scatter.6
  498.9 35.8 reduce-scatter.10
  536.2 36.5 all-gather.16
  579.2 35.7 reduce-scatter.14
  649.1 38.6 all-gather.20
  846.5 41.9 all-gather.24
  986.4 37.7 reduce-scatter.8
  1039.7 37.7 reduce-scatter.12
  1091.8 37.7 reduce-scatter.16

commit v2 on v1

--- a/solution.py
+++ b/solution.py
@@ -53,7 +53,8 @@
         return carry
 
     lax.fori_loop(0, half_rows // step, norm, 0)
-    for copy in copies:
+    early = 2 * blocks
+    for copy in copies[:early]:
         copy.wait()
 
     n_parts = 2 * blocks
@@ -71,13 +72,22 @@
             total = term if total is None else total + term
         return total
 
+    n_cols = f_cols // tile
+
+    def project_ffn(i, carry):
+        rows = pl.ds(pl.multiple_of(lax.div(i, n_cols) * tile, tile), tile)
+        cols = pl.ds(pl.multiple_of(lax.rem(i, n_cols) * tile, tile), tile)
+        gate = product(rows, wg_ref, cols)
+        up = product(rows, wu_ref, cols)
+        both_ref[rows, cols] = (gate * (1.0 / (1.0 + jnp.exp(-gate))) * up).astype(jnp.bfloat16)
+        return carry
+
+    lax.fori_loop(0, h_ref.shape[1] // tile * n_cols, project_ffn, 0)
+    for copy in copies[early:]:
+        copy.wait()
+
     def project(r, carry):
         rows = pl.ds(pl.multiple_of(r * tile, tile), tile)
-        for n in range(0, f_cols, tile):
-            cols = pl.ds(n, tile)
-            gate = product(rows, wg_ref, cols)
-            up = product(rows, wu_ref, cols)
-            both_ref[rows, cols] = (gate * (1.0 / (1.0 + jnp.exp(-gate))) * up).astype(jnp.bfloat16)
         cos_t = jnp.concatenate([cos_ref[...]] * (tile // cos_ref.shape[0]), axis=0)
         sin_t = jnp.concatenate([sin_ref[...]] * (tile // sin_ref.shape[0]), axis=0)
         rotary = lambda u: (u * cos_t + pltpu.roll(u, half_dim, 1) * sin_t).astype(jnp.bfloat16)
@@ -130,9 +140,12 @@
     half_rows = keep_ref.shape[1]
     part = w_ref.shape[-1] // 2
     tile = 256
-    for p in range(pieces):
-        for copy in copies[p]:
-            copy.wait()
+
+    def piece(p, carry):
+        for i, first in enumerate((0, pieces)):
+            depth = weights[first].shape[0]
+            start = i * weights[0].shape[0]
+            pltpu.make_async_copy(weights[first], w_ref.at[p, pl.ds(start, depth), :], sems.at[i, p]).wait()
         for j in range(2):
             block = order_ref[2 * p + j]
             for n in range(0, part, tile):
@@ -141,6 +154,9 @@
                 for dst, base in ((send_ref, half_rows), (keep_ref, 0)):
                     out = jnp.dot(both_ref[base:base + half_rows, :], w, preferred_element_type=jnp.float32)
                     dst[lax.div(block, 2), :, cols] = out.astype(jnp.bfloat16)
+        return carry
+
+    lax.fori_loop(0, pieces, piece, 0)
 
 
 def up_call(order, lens, mine, other, scale, cos_t, sin_t, gate, up, query, kv):

time: 1160 us -> 1160 us (level)
  no operation moved by 1% of the time
where the time goes in v2:
time: 1160 us; the launch traced here: 1150 us
  waiting for transfers between devices  656 us (57%)
  Pallas kernels  235 us (20%)
  other arithmetic  81.1 us (7%)
  starting transfers between devices  77 us (7%)
  local copies, waits for them, and re-layouts  72.7 us (6%)
  between operations  15.7 us (1%)
    ppermute x50, waiting for transfers between devices, send(): return lax.ppermute(value, 'bx', self.perm)  589 us
    pallas_call x6, Pallas kernels, up_call(): pl.pallas_call(functools.partial(up_kernel, head_dim), out_shape=(jax.Sha...  164 us
    pallas_call x6, Pallas kernels, down_call(): pl.pallas_call(down_kernel, out_shape=(shape, shape), in_specs=[smem, vme...  71.1 us
    ppermute x50, starting transfers between devices, send(): return lax.ppermute(value, 'bx', self.perm)  47.6 us
    ppermute x26, waiting for transfers between devices, swap_core(): return lax.ppermute(value, 'bx', core_perm)  33.4 us
    reduce_scatter x6, waiting for transfers between devices, device_program(): reduced = lax.psum_scatter(ordered, 'm', scatter_dimension=0)  32.2 us
    convert_element_type x6, other arithmetic, device_program(): (keep.astype(jnp.float32) + from_core.astype(jnp.float32)).astype(jnp.bfl...  29.4 us
    squeeze x10, local copies, waits for them, and re-layouts, take(): return lax.dynamic_slice(w, starts, [1] + sizes + list(tail))[0]  28.1 us
  transfers between devices with their start and end apart: 88, of which 34 were waited for; matrix products, arithmetic and copies ran while one was open for 12% of the time, Pallas kernels for 20%

profile of v2, /device:TPU:97, one launch (start us, length us, event | category | flops | bytes accessed | tf_op | source)
XLA Modules:
  0.0 1149.0 jit_solution(4040626950711205617)
XLA Ops:
  8.6 3.8 collective-permute-start.2
  12.4 8.3 collective-permute-done.2
  23.4 3.0 collective-permute-start.16
  26.4 3.4 dynamic-slice_bitcast_fusion.7
  31.5 2.7 collective-permute-start.60
  34.2 4.2 dynamic-slice_bitcast_fusion.2
  38.4 4.5 dynamic-slice_bitcast_fusion.1
  47.7 2.9 dynamic-slice_bitcast_fusion.24
  50.6 3.8 dynamic-slice_bitcast_fusion
  55.0 2.9 dynamic-slice_bitcast_fusion.22
  58.8 6.0 collective-permute-done.30
  82.6 30.5 %collective-permute-done.68 = bf16[128,1536]{1,0:T(8,128)(2,1)S(1)} collective-permute-done((bf16[128,1536]{1,0:T(8,128)(2,1)S(1)}, bf16[128,1536]{1,0:T(8,128)(2,1)S(1)}, u32[]{:S(2)}, u32[]{:S(2)}) %collective-permute-start.68) | collective-permute-done | bytes 393248 | tf_op jit(solution)/shard_map/ppermute | solution.py:218
  121.8 11.4 all-gather.7
  135.0 5.9 collective-permute-done.25.refs_5_
  140.8 3.3 collective-permute-start.3
  147.8 26.9 %collective-permute-done.9.refs_5_ = bf16[1536,512]{1,0:T(8,128)(2,1)} collective-permute-done((bf16[1536,512]{1,0:T(8,128)(2,1)}, bf16[1536,512]{1,0:T(8,128)(2,1)}, u32[]{:S(2)}, u32[]{:S(2)}) %collective-permute-start.9) | collective-permute-done | bytes 1572896 | tf_op jit(solution)/shard_map/ppermute | solution.py:218
  175.6 32.7 %collective-permute-done.5.refs_1_ = bf16[1536,512]{1,0:T(8,128)(2,1)} collective-permute-done((bf16[1536,512]{1,0:T(8,128)(2,1)}, bf16[1536,512]{1,0:T(8,128)(2,1)}, u32[]{:S(2)}, u32[]{:S(2)}) %collective-permute-start.5) | collective-permute-done | bytes 1572896 | tf_op jit(solution)/shard_map/ppermute | solution.py:218
  218.3 23.8 %collective-permute-done.21.refs_1_ = bf16[512,1536]{1,0:T(8,128)(2,1)} collective-permute-done((bf16[512,1536]{1,0:T(8,128)(2,1)}, bf16[512,1536]{1,0:T(8,128)(2,1)}, u32[]{:S(2)}, u32[]{:S(2)}) %collective-permute-start.21) | collective-permute-done | bytes 1572896 | tf_op jit(solution)/shard_map/ppermute | solution.py:218
  245.2 21.4 %collective-permute-done.11.refs_7_ = bf16[1536,512]{1,0:T(8,128)(2,1)} collective-permute-done((bf16[1536,512]{1,0:T(8,128)(2,1)}, bf16[1536,512]{1,0:T(8,128)(2,1)}, u32[]{:S(2)}, u32[]{:S(2)}) %collective-permute-start.11) | collective-permute-done | bytes 1572896 | tf_op jit(solution)/shard_map/ppermute | solution.py:218
  266.9 33.4 %collective-permute-done.7.refs_3_ = bf16[1536,512]{1,0:T(8,128)(2,1)} collective-permute-done((bf16[1536,512]{1,0:T(8,128)(2,1)}, bf16[1536,512]{1,0:T(8,128)(2,1)}, u32[]{:S(2)}, u32[]{:S(2)}) %collective-permute-start.7) | collective-permute-done | bytes 1572896 | tf_op jit(solution)/shard_map/ppermute | solution.py:218
  302.3 27.4 %shard_map.121 = (bf16[512,896]{1,0:T(8,128)(2,1)}, bf16[128,128]{1,0:T(8,128)(2,1)}, bf16[128,128]{1,0:T(8,128)(2,1)}) custom-call(s32[8]{0:T(128)} %convert_element_type.168.order_ref, s32[4]{0:T(128)} %reshape_squeeze.18.lens_ref, bf16[4,256,1536]{2,1,0:T(8,128)(2,1)} %bitcast.254, bf16[4,256,1536]{2,1,0:T(8,128)(2,1)} %collective-permute-done.3.other_ref, ...), custom_call_target="tpu_custom_call" | custom-call | flops 10468982784 | bytes 26738688 | tf_op jit(solution)/shard_map/pallas_call | solution.py:171
  329.6 63.3 %collective-permute-done.26.refs_6_ = bf16[384,1536]{1,0:T(8,128)(2,1)S(1)} collective-permute-done((bf16[384,1536]{1,0:T(8,128)(2,1)S(1)}, bf16[384,1536]{1,0:T(8,128)(2,1)S(1)}, u32[]{:S(2)}, u32[]{:S(2)}) %collective-permute-start.26) | collective-permute-done | bytes 1179680 | tf_op jit(solution)/shard_map/ppermute | solution.py:218
  392.9 25.4 %collective-permute-done.27.refs_7_ = bf16[384,1536]{1,0:T(8,128)(2,1)} collective-permute-done((bf16[384,1536]{1,0:T(8,128)(2,1)S(1)}, bf16[384,1536]{1,0:T(8,128)(2,1)}, u32[]{:S(2)}, u32[]{:S(2)}) %collective-permute-start.27) | collective-permute-done | bytes 1179680 | tf_op jit(solution)/shard_map/ppermute | solution.py:218
  419.5 11.8 %shard_map.122 = (bf16[4,256,1536]{2,1,0:T(8,128)(2,1)}, bf16[4,256,1536]{2,1,0:T(8,128)(2,1)}) custom-call(s32[8]{0:T(128)S(1)} %copy-done, bf16[512,896]{1,0:T(8,128)(2,1)S(1)} %copy-done.8, bf16[512,1536]{1,0:T(8,128)(2,1)} %pad_maximum_fusion.7.refs_0_, bf16[512,1536]{1,0:T(8,128)(2,1)} %collective-permute-done.21.refs_1_, ...), custom_call_target="tpu_custom_call" | custom-call | flops 5637144576 | bytes 17301504 | tf_op jit(solution)/shard_map/pallas_call | solution.py:197
  431.3 4.3 collective-permute-start.28
  435.7 5.5 collective-permute-done.28
  441.2 5.4 add_convert_fusion.5
  447.6 27.4 %shard_map.125 = (bf16[512,896]{1,0:T(8,128)(2,1)}, bf16[128,128]{1,0:T(8,128)(2,1)}, bf16[128,128]{1,0:T(8,128)(2,1)}) custom-call(s32[8]{0:T(128)} %convert_element_type.168.order_ref, s32[4]{0:T(128)} %reshape_squeeze.20.lens_ref, bf16[4,256,1536]{2,1,0:T(8,128)(2,1)} %bitcast.258, bf16[4,256,1536]{2,1,0:T(8,128)(2,1)} %collective-permute-done.61.other_ref, ...), custom_call_target="tpu_custom_call" | custom-call | flops 10468982784 | bytes 26738688 | tf_op jit(solution)/shard_map/pallas_call | solution.py:171
  476.2 11.9 %shard_map.126 = (bf16[4,256,1536]{2,1,0:T(8,128)(2,1)}, bf16[4,256,1536]{2,1,0:T(8,128)(2,1)}) custom-call(s32[8]{0:T(128)S(1)} %copy-done.1, bf16[512,896]{1,0:T(8,128)(2,1)S(1)} %copy-done.10, bf16[512,1536]{1,0:T(8,128)(2,1)} %pad_maximum_fusion.7.refs_0_, bf16[512,1536]{1,0:T(8,128)(2,1)} %collective-permute-done.21.refs_1_, ...), custom_call_target="tpu_custom_call" | custom-call | flops 5637144576 | bytes 17301504 | tf_op jit(solution)/shard_map/pallas_call | solution.py:197
  488.5 5.5 collective-permute-done.62
  494.0 4.5 add_convert_fusion.3
  500.5 11.5 %collective-permute-done.29 = bf16[128,1536]{1,0:T(8,128)(2,1)S(1)} collective-permute-done((bf16[128,1536]{1,0:T(8,128)(2,1)S(1)}, bf16[128,1536]{1,0:T(8,128)(2,1)S(1)}, u32[]{:S(2)}, u32[]{:S(2)}) %collective-permute-start.29) | collective-permute-done | bytes 393248 | tf_op jit(solution)/shard_map/ppermute | solution.py:218
  514.7 9.5 collective-permute-done.32
  526.9 27.4 %shard_map.129 = (bf16[512,896]{1,0:T(8,128)(2,1)}, bf16[128,128]{1,0:T(8,128)(2,1)}, bf16[128,128]{1,0:T(8,128)(2,1)}) custom-call(s32[8]{0:T(128)} %convert_element_type.168.order_ref, s32[4]{0:T(128)} %reshape_squeeze.22.lens_ref, bf16[4,256,1536]{2,1,0:T(8,128)(2,1)} %bitcast.262, bf16[4,256,1536]{2,1,0:T(8,128)(2,1)} %collective-permute-done.69.other_ref, ...), custom_call_target="tpu_custom_call" | custom-call | flops 10468982784 | bytes 26738688 | tf_op jit(solution)/shard_map/pallas_call | solution.py:171
  555.5 11.9 %shard_map.130 = (bf16[4,256,1536]{2,1,0:T(8,128)(2,1)}, bf16[4,256,1536]{2,1,0:T(8,128)(2,1)}) custom-call(s32[8]{0:T(128)S(1)} %copy-done.2, bf16[512,896]{1,0:T(8,128)(2,1)S(1)} %copy-done.7, bf16[512,1536]{1,0:T(8,128)(2,1)} %pad_maximum_fusion.7.refs_0_, bf16[512,1536]{1,0:T(8,128)(2,1)} %collective-permute-done.21.refs_1_, ...), custom_call_target="tpu_custom_call" | custom-call | flops 5637144576 | bytes 17301504 | tf_op jit(solution)/shard_map/pallas_call | solution.py:197
  569.2 5.5 collective-permute-done.70
  574.7 4.4 add_convert_fusion.1
  581.3 10.2 collective-permute-done.46
  593.7 8.9 collective-permute-done.48
  613.1 7.3 collective-permute-done.63
  623.8 3.4 constant_dynamic-slice_fusion.6
  627.1 18.9 %collective-permute-done.64 = bf16[128,1536]{1,0:T(8,128)(2,1)S(1)} collective-permute-done((bf16[128,1536]{1,0:T(8,128)(2,1)S(1)}, bf16[128,1536]{1,0:T(8,128)(2,1)S(1)}, u32[]{:S(2)}, u32[]{:S(2)}) %collective-permute-start.64) | collective-permute-done | bytes 393248 | tf_op jit(solution)/shard_map/ppermute | solution.py:218
  661.8 17.6 %collective-permute-done.55.refs_5_ = bf16[384,1536]{1,0:T(8,128)(2,1)S(1)} collective-permute-done((bf16[384,1536]{1,0:T(8,128)(2,1)S(1)}, bf16[384,1536]{1,0:T(8,128)(2,1)S(1)}, u32[]{:S(2)}, u32[]{:S(2)}) %collective-permute-start.55) | collective-permute-done | bytes 1179680 | tf_op jit(solution)/shard_map/ppermute | solution.py:218
  682.4 30.7 %collective-permute-done.35.refs_1_ = bf16[1536,512]{1,0:T(8,128)(2,1)} collective-permute-done((bf16[1536,512]{1,0:T(8,128)(2,1)}, bf16[1536,512]{1,0:T(8,128)(2,1)}, u32[]{:S(2)}, u32[]{:S(2)}) %collective-permute-start.35) | collective-permute-done | bytes 1572896 | tf_op jit(solution)/shard_map/ppermute | solution.py:218
  717.8 29.0 %collective-permute-done.39.refs_5_ = bf16[1536,512]{1,0:T(8,128)(2,1)} collective-permute-done((bf16[1536,512]{1,0:T(8,128)(2,1)}, bf16[1536,512]{1,0:T(8,128)(2,1)}, u32[]{:S(2)}, u32[]{:S(2)}) %collective-permute-start.39) | collective-permute-done | bytes 1572896 | tf_op jit(solution)/shard_map/ppermute | solution.py:218
  760.9 21.3 %collective-permute-done.51.refs_1_ = bf16[512,1536]{1,0:T(8,128)(2,1)} collective-permute-done((bf16[512,1536]{1,0:T(8,128)(2,1)}, bf16[512,1536]{1,0:T(8,128)(2,1)}, u32[]{:S(2)}, u32[]{:S(2)}) %collective-permute-start.51) | collective-permute-done | bytes 1572896 | tf_op jit(solution)/shard_map/ppermute | solution.py:218
  784.6 23.8 %collective-permute-done.45.refs_11_ = bf16[3,1536,128]{2,1,0:T(8,128)(2,1)S(1)} collective-permute-done((bf16[3,1536,128]{2,1,0:T(8,128)(2,1)}, bf16[3,1536,128]{2,1,0:T(8,128)(2,1)S(1)}, u32[]{:S(2)}, u32[]{:S(2)}) %collective-permute-start.45) | collective-permute-done | bytes 1179680 | tf_op jit(solution)/shard_map/ppermute | solution.py:218
  812.4 29.7 %collective-permute-done.41.refs_7_ = bf16[1536,512]{1,0:T(8,128)(2,1)S(1)} collective-permute-done((bf16[1536,512]{1,0:T(8,128)(2,1)}, bf16[1536,512]{1,0:T(8,128)(2,1)S(1)}, u32[]{:S(2)}, u32[]{:S(2)}) %collective-permute-start.41) | collective-permute-done | bytes 1572896 | tf_op jit(solution)/shard_map/ppermute | solution.py:218
  846.6 27.4 %shard_map.123 = (bf16[512,896]{1,0:T(8,128)(2,1)}, bf16[128,128]{1,0:T(8,128)(2,1)}, bf16[128,128]{1,0:T(8,128)(2,1)}) custom-call(s32[8]{0:T(128)} %convert_element_type.178.order_ref, s32[4]{0:T(128)} %reshape_squeeze.19.lens_ref, bf16[4,256,1536]{2,1,0:T(8,128)(2,1)} %bitcast.256, bf16[4,256,1536]{2,1,0:T(8,128)(2,1)} %collective-permute-done.33.other_ref, ...), custom_call_target="tpu_custom_call" | custom-call | flops 10468982784 | bytes 26738688 | tf_op jit(solution)/shard_map/pallas_call | solution.py:171
  874.0 60.7 %collective-permute-done.56.refs_6_ = bf16[384,1536]{1,0:T(8,128)(2,1)S(1)} collective-permute-done((bf16[384,1536]{1,0:T(8,128)(2,1)S(1)}, bf16[384,1536]{1,0:T(8,128)(2,1)S(1)}, u32[]{:S(2)}, u32[]{:S(2)}) %collective-permute-start.56) | collective-permute-done | bytes 1179680 | tf_op jit(solution)/shard_map/ppermute | solution.py:218
  934.7 25.4 %collective-permute-done.57.refs_7_ = bf16[384,1536]{1,0:T(8,128)(2,1)} collective-permute-done((bf16[384,1536]{1,0:T(8,128)(2,1)S(1)}, bf16[384,1536]{1,0:T(8,128)(2,1)}, u32[]{:S(2)}, u32[]{:S(2)}) %collective-permute-start.57) | collective-permute-done | bytes 1179680 | tf_op jit(solution)/shard_map/ppermute | solution.py:218
  961.3 11.8 %shard_map.124 = (bf16[4,256,1536]{2,1,0:T(8,128)(2,1)}, bf16[4,256,1536]{2,1,0:T(8,128)(2,1)}) custom-call(s32[8]{0:T(128)S(1)} %copy-done.3, bf16[512,896]{1,0:T(8,128)(2,1)S(1)} %copy-done.9, bf16[512,1536]{1,0:T(8,128)(2,1)} %pad_maximum_fusion.14.refs_0_, bf16[512,1536]{1,0:T(8,128)(2,1)} %collective-permute-done.51.refs_1_, ...), custom_call_target="tpu_custom_call" | custom-call | flops 5637144576 | bytes 17301504 | tf_op jit(solution)/shard_map/pallas_call | solution.py:197
  975.4 5.5 collective-permute-done.58
  980.9 5.4 add_convert_fusion.4
  987.2 27.4 %shard_map.127 = (bf16[512,896]{1,0:T(8,128)(2,1)}, bf16[128,128]{1,0:T(8,128)(2,1)}, bf16[128,128]{1,0:T(8,128)(2,1)}) custom-call(s32[8]{0:T(128)} %convert_element_type.178.order_ref, s32[4]{0:T(128)} %reshape_squeeze.21.lens_ref, bf16[4,256,1536]{2,1,0:T(8,128)(2,1)} %bitcast.260, bf16[4,256,1536]{2,1,0:T(8,128)(2,1)} %collective-permute-done.65.other_ref, ...), custom_call_target="tpu_custom_call" | custom-call | flops 10468982784 | bytes 26738688 | tf_op jit(solution)/shard_map/pallas_call | solution.py:171
  1015.8 11.9 %shard_map.128 = (bf16[4,256,1536]{2,1,0:T(8,128)(2,1)}, bf16[4,256,1536]{2,1,0:T(8,128)(2,1)}) custom-call(s32[8]{0:T(128)S(1)} %copy-done.4, bf16[512,896]{1,0:T(8,128)(2,1)S(1)} %copy-done.11, bf16[512,1536]{1,0:T(8,128)(2,1)} %pad_maximum_fusion.14.refs_0_, bf16[512,1536]{1,0:T(8,128)(2,1)} %collective-permute-done.51.refs_1_, ...), custom_call_target="tpu_custom_call" | custom-call | flops 5637144576 | bytes 17301504 | tf_op jit(solution)/shard_map/pallas_call | solution.py:197
  1028.3 5.5 collective-permute-done.66
  1033.8 5.4 add_convert_fusion.2
  1040.2 27.4 %shard_map.131 = (bf16[512,896]{1,0:T(8,128)(2,1)}, bf16[128,128]{1,0:T(8,128)(2,1)}, bf16[128,128]{1,0:T(8,128)(2,1)}) custom-call(s32[8]{0:T(128)} %convert_element_type.178.order_ref, s32[4]{0:T(128)} %reshape_squeeze.23.lens_ref, bf16[4,256,1536]{2,1,0:T(8,128)(2,1)} %bitcast.264, bf16[4,256,1536]{2,1,0:T(8,128)(2,1)} %collective-permute-done.73.other_ref, ...), custom_call_target="tpu_custom_call" | custom-call | flops 10468982784 | bytes 26738688 | tf_op jit(solution)/shard_map/pallas_call | solution.py:171
  1068.7 11.8 %shard_map.132 = (bf16[4,256,1536]{2,1,0:T(8,128)(2,1)}, bf16[4,256,1536]{2,1,0:T(8,128)(2,1)}) custom-call(s32[8]{0:T(128)S(1)} %copy-done.5, bf16[512,896]{1,0:T(8,128)(2,1)S(1)} %copy-done.6, bf16[512,1536]{1,0:T(8,128)(2,1)} %pad_maximum_fusion.14.refs_0_, bf16[512,1536]{1,0:T(8,128)(2,1)} %collective-permute-done.51.refs_1_, ...), custom_call_target="tpu_custom_call" | custom-call | flops 5637144576 | bytes 17301504 | tf_op jit(solution)/shard_map/pallas_call | solution.py:197
  1081.0 5.5 collective-permute-done.74
  1086.5 4.4 add_convert_fusion
  1097.2 32.2 %reduce-scatter.17.cloned.1.call-done = bf16[1,256,1536]{2,1,0:T(8,128)(2,1)} async-done(((bf16[4,256,1536]{2,1,0:T(8,128)(2,1)}), bf16[1,256,1536]{2,1,0:T(8,128)(2,1)}) %reduce-scatter.17.cloned.1.call-update) | async-done | bytes 786448 | tf_op jit(solution)/shard_map/reduce_scatter | solution.py:307
  1133.0 7.4 collective-permute-done.75
  (414 shorter events, 160.6 us)
Async XLA Ops:
  7.2 133.7 %all-gather.15.cloned.1.call-start = ((), (), s32[]{:S(2)}) async-start(), calls=%async_computation.12 | async-start | bytes 3932160 | tf_op jit(solution)/shard_map/all_gather | solution.py:299
  21.7 413.9 %all-gather.19.cloned.1.call-start = ((), (), s32[]{:S(2)}) async-start(), calls=%async_computation.14 | async-start | bytes 3932160 | tf_op jit(solution)/shard_map/all_gather | solution.py:299
  23.4 31.0 %collective-permute-start.16 = (bf16[768,256]{1,0:T(8,128)(2,1)}, bf16[768,256]{1,0:T(8,128)(2,1)}, u32[]{:S(2)}, u32[]{:S(2)}) collective-permute-start(bf16[768,256]{1,0:T(8,128)(2,1)} %get-tuple-element.137), channel_id=1, source_target_pairs={{0,6},{1,7},{2,4},{3,5},{4,2},{5,3},{6,0},{7,1},{8,14},{9,15},{10,... | collective-permute-start | bytes 1179656 | tf_op jit(solution)/shard_map/ppermute | solution.py:218
  26.4 39.9 %collective-permute-start.17 = (bf16[768,256]{1,0:T(8,128)(2,1)}, bf16[768,256]{1,0:T(8,128)(2,1)}, u32[]{:S(2)}, u32[]{:S(2)}) collective-permute-start(bf16[768,256]{1,0:T(8,128)(2,1)} %get-tuple-element.137), channel_id=1, source_target_pairs={{0,2},{1,3},{2,0},{3,1},{4,6},{5,7},{6,4},{7,5},{8,10},{9,11},{10,... | collective-permute-start | bytes 1179656 | tf_op jit(solution)/shard_map/ppermute | solution.py:218
  29.8 41.3 %collective-permute-start.12 = (bf16[6,768,128]{2,1,0:T(8,128)(2,1)}, bf16[6,768,128]{2,1,0:T(8,128)(2,1)}, u32[]{:S(2)}, u32[]{:S(2)}) collective-permute-start(bf16[6,768,128]{2,1,0:T(8,128)(2,1)} %get-tuple-element.98), channel_id=1, source_target_pairs={{0,1},{1,0},{2,3},{3,2},{4,5},{5,4},{6,7},{7,6},{8,9},{9,8},{10,11... | collective-permute-start | bytes 3538952 | tf_op jit(solution)/shard_map/ppermute | solution.py:231
  31.5 26.4 %collective-permute-start = (s32[3]{0:T(128)S(1)}, s32[3]{0:T(128)S(1)}, u32[]{:S(2)}, u32[]{:S(2)}) collective-permute-start(s32[3]{0:T(128)S(1)} %copy-done.73), channel_id=1, source_target_pairs={{0,6},{1,7},{2,4},{3,5},{4,2},{5,3},{6,0},{7,1},{8,14},{9,15},{10,... | collective-permute-start | bytes 44 | tf_op jit(solution)/shard_map/ppermute | solution.py:218
  31.5 34.8 %collective-permute-start.60 = (bf16[128,1536]{1,0:T(8,128)(2,1)S(1)}, bf16[128,1536]{1,0:T(8,128)(2,1)}, u32[]{:S(2)}, u32[]{:S(2)}) collective-permute-start(bf16[128,1536]{1,0:T(8,128)(2,1)S(1)} %get-tuple-element.121), channel_id=1, source_target_pairs={{0,6},{1,7},{2,4},{3,5},{4,2},{5,3},{6,0},{7,1},{8,14},{9,15},{10,... | collective-permute-start | bytes 1179656 | tf_op jit(solution)/shard_map/ppermute | solution.py:218
  54.4 15.1 %collective-permute-start.18 = (bf16[768,256]{1,0:T(8,128)(2,1)}, bf16[768,256]{1,0:T(8,128)(2,1)S(1)}, u32[]{:S(2)}, u32[]{:S(2)}) collective-permute-start(bf16[768,256]{1,0:T(8,128)(2,1)} %collective-permute-done.16), channel_id=1, source_target_pairs={{0,2},{1,3},{2,0},{3,1},{4,6},{5,7},{6,4},{7,5},{8,10},{9,11},{10,... | collective-permute-start | bytes 1179656 | tf_op jit(solution)/shard_map/ppermute | solution.py:218
  68.7 429.9 %all-gather.23.cloned.1.call-start = ((), (), s32[]{:S(2)}) async-start(), calls=%async_computation.16 | async-start | bytes 3932160 | tf_op jit(solution)/shard_map/all_gather | solution.py:299
  69.5 43.9 %collective-permute-start.20 = (bf16[1024,768]{1,0:T(8,128)(2,1)}, bf16[1024,768]{1,0:T(8,128)(2,1)S(1)}, u32[]{:S(2)}, u32[]{:S(2)}) collective-permute-start(bf16[1024,768]{1,0:T(8,128)(2,1)} %get-tuple-element.74), channel_id=1, source_target_pairs={{0,1},{1,0},{2,3},{3,2},{4,5},{5,4},{6,7},{7,6},{8,9},{9,8},{10,11... | collective-permute-start | bytes 4718600 | tf_op jit(solution)/shard_map/ppermute | solution.py:231
  73.5 46.8 %collective-permute-start.19 = (bf16[4,768,256]{2,1,0:T(8,128)(2,1)S(1)}, bf16[4,768,256]{2,1,0:T(8,128)(2,1)S(1)}, u32[]{:S(2)}, u32[]{:S(2)}) collective-permute-start(bf16[4,768,256]{2,1,0:T(8,128)(2,1)S(1)} %pad_maximum_fusion.6), channel_id=1, source_target_pairs={{0,1},{1,0},{2,3},{3,2},{4,5},{5,4},{6,7},{7,6},{8,9},{9,8},{10,11... | collective-permute-start | bytes 4718600 | tf_op jit(solution)/shard_map/ppermute | solution.py:231
  76.1 42.4 %collective-permute-start.13 = (bf16[3,1536,128]{2,1,0:T(8,128)(2,1)S(1)}, bf16[3,1536,128]{2,1,0:T(8,128)(2,1)}, u32[]{:S(2)}, u32[]{:S(2)}) collective-permute-start(bf16[3,1536,128]{2,1,0:T(8,128)(2,1)S(1)} %pad_maximum_fusion.17), channel_id=1, source_target_pairs={{0,6},{1,7},{2,4},{3,5},{4,2},{5,3},{6,0},{7,1},{8,14},{9,15},{10,... | collective-permute-start | bytes 3538952 | tf_op jit(solution)/shard_map/ppermute | solution.py:218
  76.5 36.6 %collective-permute-start.68 = (bf16[128,1536]{1,0:T(8,128)(2,1)S(1)}, bf16[128,1536]{1,0:T(8,128)(2,1)S(1)}, u32[]{:S(2)}, u32[]{:S(2)}) collective-permute-start(bf16[128,1536]{1,0:T(8,128)(2,1)S(1)} %get-tuple-element.120), channel_id=1, source_target_pairs={{0,6},{1,7},{2,4},{3,5},{4,2},{5,3},{6,0},{7,1},{8,14},{9,15},{10,... | collective-permute-start | bytes 1179656 | tf_op jit(solution)/shard_map/ppermute | solution.py:218
  79.0 41.4 %collective-permute-start.14 = (bf16[3,1536,128]{2,1,0:T(8,128)(2,1)S(1)}, bf16[3,1536,128]{2,1,0:T(8,128)(2,1)S(1)}, u32[]{:S(2)}, u32[]{:S(2)}) collective-permute-start(bf16[3,1536,128]{2,1,0:T(8,128)(2,1)S(1)} %pad_maximum_fusion.16.refs_8_), channel_id=1, source_target_pairs={{0,2},{1,3},{2,0},{3,1},{4,6},{5,7},{6,4},{7,5},{8,10},{9,11},{10,... | collective-permute-start | bytes 3538952 | tf_op jit(solution)/shard_map/ppermute | solution.py:218
  113.1 27.7 %collective-permute-start.25 = (bf16[384,1536]{1,0:T(8,128)(2,1)S(1)}, bf16[384,1536]{1,0:T(8,128)(2,1)S(1)}, u32[]{:S(2)}, u32[]{:S(2)}) collective-permute-start(bf16[384,1536]{1,0:T(8,128)(2,1)S(1)} %pad_maximum_fusion.19), channel_id=1, source_target_pairs={{0,6},{1,7},{2,4},{3,5},{4,2},{5,3},{6,0},{7,1},{8,14},{9,15},{10,... | collective-permute-start | bytes 3538952 | tf_op jit(solution)/shard_map/ppermute | solution.py:218
  113.4 61.2 %collective-permute-start.9 = (bf16[1536,512]{1,0:T(8,128)(2,1)}, bf16[1536,512]{1,0:T(8,128)(2,1)}, u32[]{:S(2)}, u32[]{:S(2)}) collective-permute-start(bf16[1536,512]{1,0:T(8,128)(2,1)} %pad_maximum_fusion.5), channel_id=1, source_target_pairs={{0,6},{1,7},{2,4},{3,5},{4,2},{5,3},{6,0},{7,1},{8,14},{9,15},{10,... | collective-permute-start | bytes 4718600 | tf_op jit(solution)/shard_map/ppermute | solution.py:218
  118.5 89.9 %collective-permute-start.5 = (bf16[1536,512]{1,0:T(8,128)(2,1)}, bf16[1536,512]{1,0:T(8,128)(2,1)}, u32[]{:S(2)}, u32[]{:S(2)}) collective-permute-start(bf16[1536,512]{1,0:T(8,128)(2,1)} %pad_maximum_fusion.3), channel_id=1, source_target_pairs={{0,6},{1,7},{2,4},{3,5},{4,2},{5,3},{6,0},{7,1},{8,14},{9,15},{10,... | collective-permute-start | bytes 4718600 | tf_op jit(solution)/shard_map/ppermute | solution.py:218
  120.3 89.3 %collective-permute-start.10 = (bf16[1536,512]{1,0:T(8,128)(2,1)}, bf16[1536,512]{1,0:T(8,128)(2,1)}, u32[]{:S(2)}, u32[]{:S(2)}) collective-permute-start(bf16[1536,512]{1,0:T(8,128)(2,1)} %pad_maximum_fusion.4.refs_4_), channel_id=1, source_target_pairs={{0,2},{1,3},{2,0},{3,1},{4,6},{5,7},{6,4},{7,5},{8,10},{9,11},{10,... | collective-permute-start | bytes 4718600 | tf_op jit(solution)/shard_map/ppermute | solution.py:218
  120.4 90.7 %collective-permute-start.6 = (bf16[1536,512]{1,0:T(8,128)(2,1)}, bf16[1536,512]{1,0:T(8,128)(2,1)}, u32[]{:S(2)}, u32[]{:S(2)}) collective-permute-start(bf16[1536,512]{1,0:T(8,128)(2,1)} %pad_maximum_fusion.2.refs_0_), channel_id=1, source_target_pairs={{0,2},{1,3},{2,0},{3,1},{4,6},{5,7},{6,4},{7,5},{8,10},{9,11},{10,... | collective-permute-start | bytes 4718600 | tf_op jit(solution)/shard_map/ppermute | solution.py:218
  140.8 161.4 %collective-permute-start.3 = (bf16[4,256,1536]{2,1,0:T(8,128)(2,1)}, bf16[4,256,1536]{2,1,0:T(8,128)(2,1)}, u32[]{:S(2)}, u32[]{:S(2)}) collective-permute-start(bf16[4,256,1536]{2,1,0:T(8,128)(2,1)} %bitcast.253), channel_id=1, source_target_pairs={{0,1},{1,0},{2,3},{3,2},{4,5},{5,4},{6,7},{7,6},{8,9},{9,8},{10,11... | collective-permute-start | bytes 9437192 | tf_op jit(solution)/shard_map/ppermute | solution.py:231
  174.6 67.4 %collective-permute-start.21 = (bf16[512,1536]{1,0:T(8,128)(2,1)}, bf16[512,1536]{1,0:T(8,128)(2,1)}, u32[]{:S(2)}, u32[]{:S(2)}) collective-permute-start(bf16[512,1536]{1,0:T(8,128)(2,1)} %pad_maximum_fusion.8), channel_id=1, source_target_pairs={{0,6},{1,7},{2,4},{3,5},{4,2},{5,3},{6,0},{7,1},{8,14},{9,15},{10,... | collective-permute-start | bytes 4718600 | tf_op jit(solution)/shard_map/ppermute | solution.py:218
  208.4 33.7 %collective-permute-start.15 = (bf16[3,1536,128]{2,1,0:T(8,128)(2,1)}, bf16[3,1536,128]{2,1,0:T(8,128)(2,1)}, u32[]{:S(2)}, u32[]{:S(2)}) collective-permute-start(bf16[3,1536,128]{2,1,0:T(8,128)(2,1)} %collective-permute-done.13.refs_9_), channel_id=1, source_target_pairs={{0,2},{1,3},{2,0},{3,1},{4,6},{5,7},{6,4},{7,5},{8,10},{9,11},{10,... | collective-permute-start | bytes 3538952 | tf_op jit(solution)/shard_map/ppermute | solution.py:218
  209.6 57.0 %collective-permute-start.11 = (bf16[1536,512]{1,0:T(8,128)(2,1)}, bf16[1536,512]{1,0:T(8,128)(2,1)}, u32[]{:S(2)}, u32[]{:S(2)}) collective-permute-start(bf16[1536,512]{1,0:T(8,128)(2,1)} %collective-permute-done.9.refs_5_), channel_id=1, source_target_pairs={{0,2},{1,3},{2,0},{3,1},{4,6},{5,7},{6,4},{7,5},{8,10},{9,11},{10,... | collective-permute-start | bytes 4718600 | tf_op jit(solution)/shard_map/ppermute | solution.py:218
  211.1 89.2 %collective-permute-start.7 = (bf16[1536,512]{1,0:T(8,128)(2,1)}, bf16[1536,512]{1,0:T(8,128)(2,1)}, u32[]{:S(2)}, u32[]{:S(2)}) collective-permute-start(bf16[1536,512]{1,0:T(8,128)(2,1)} %collective-permute-done.5.refs_1_), channel_id=1, source_target_pairs={{0,2},{1,3},{2,0},{3,1},{4,6},{5,7},{6,4},{7,5},{8,10},{9,11},{10,... | collective-permute-start | bytes 4718600 | tf_op jit(solution)/shard_map/ppermute | solution.py:218
  214.1 285.0 %reduce-scatter.7.cloned.1.call-start = ((), (), s32[]{:S(2)}) async-start(), calls=%async_computation.6 | async-start | bytes 3932160 | tf_op jit(solution)/shard_map/reduce_scatter | solution.py:307
  242.1 150.8 %collective-permute-start.22 = (bf16[512,1536]{1,0:T(8,128)(2,1)}, bf16[512,1536]{1,0:T(8,128)(2,1)}, u32[]{:S(2)}, u32[]{:S(2)}) collective-permute-start(bf16[512,1536]{1,0:T(8,128)(2,1)} %pad_maximum_fusion.7.refs_0_), channel_id=1, source_target_pairs={{0,2},{1,3},{2,0},{3,1},{4,6},{5,7},{6,4},{7,5},{8,10},{9,11},{10,... | collective-permute-start | bytes 4718600 | tf_op jit(solution)/shard_map/ppermute | solution.py:218
  242.1 176.2 %collective-permute-start.23 = (bf16[512,1536]{1,0:T(8,128)(2,1)}, bf16[512,1536]{1,0:T(8,128)(2,1)}, u32[]{:S(2)}, u32[]{:S(2)}) collective-permute-start(bf16[512,1536]{1,0:T(8,128)(2,1)} %collective-permute-done.21.refs_1_), channel_id=1, source_target_pairs={{0,2},{1,3},{2,0},{3,1},{4,6},{5,7},{6,4},{7,5},{8,10},{9,11},{10,... | collective-permute-start | bytes 4718600 | tf_op jit(solution)/shard_map/ppermute | solution.py:218
  266.6 126.3 %collective-permute-start.26 = (bf16[384,1536]{1,0:T(8,128)(2,1)S(1)}, bf16[384,1536]{1,0:T(8,128)(2,1)S(1)}, u32[]{:S(2)}, u32[]{:S(2)}) collective-permute-start(bf16[384,1536]{1,0:T(8,128)(2,1)S(1)} %pad_maximum_fusion.18.refs_4_), channel_id=1, source_target_pairs={{0,2},{1,3},{2,0},{3,1},{4,6},{5,7},{6,4},{7,5},{8,10},{9,11},{10,... | collective-permute-start | bytes 3538952 | tf_op jit(solution)/shard_map/ppermute | solution.py:218
  300.3 118.0 %collective-permute-start.27 = (bf16[384,1536]{1,0:T(8,128)(2,1)S(1)}, bf16[384,1536]{1,0:T(8,128)(2,1)}, u32[]{:S(2)}, u32[]{:S(2)}) collective-permute-start(bf16[384,1536]{1,0:T(8,128)(2,1)S(1)} %collective-permute-done.25.refs_5_), channel_id=1, source_target_pairs={{0,2},{1,3},{2,0},{3,1},{4,6},{5,7},{6,4},{7,5},{8,10},{9,11},{10,... | collective-permute-start | bytes 3538952 | tf_op jit(solution)/shard_map/ppermute | solution.py:218
  446.6 161.5 %reduce-scatter.11.cloned.1.call-start = ((), (), s32[]{:S(2)}) async-start(), calls=%async_computation.8 | async-start | bytes 3932160 | tf_op jit(solution)/shard_map/reduce_scatter | solution.py:307
  498.5 180.9 %all-gather.17.cloned.1.call-start = ((), (), s32[]{:S(2)}) async-start(), calls=%async_computation.13 | async-start | bytes 3932160 | tf_op jit(solution)/shard_map/all_gather | solution.py:299
  498.6 28.2 %collective-permute-start.69 = (bf16[4,256,1536]{2,1,0:T(8,128)(2,1)}, bf16[4,256,1536]{2,1,0:T(8,128)(2,1)}, u32[]{:S(2)}, u32[]{:S(2)}) collective-permute-start(bf16[4,256,1536]{2,1,0:T(8,128)(2,1)} %bitcast.261), channel_id=1, source_target_pairs={{0,1},{1,0},{2,3},{3,2},{4,5},{5,4},{6,7},{7,6},{8,9},{9,8},{10,11... | collective-permute-start | bytes 9437192 | tf_op jit(solution)/shard_map/ppermute | solution.py:231
  526.3 154.3 %reduce-scatter.15.cloned.1.call-start = ((), (), s32[]{:S(2)}) async-start(), calls=%async_computation.10 | async-start | bytes 3932160 | tf_op jit(solution)/shard_map/reduce_scatter | solution.py:307
  579.1 396.1 %all-gather.21.cloned.1.call-start = ((), (), s32[]{:S(2)}) async-start(), calls=%async_computation.15 | async-start | bytes 3932160 | tf_op jit(solution)/shard_map/all_gather | solution.py:299
  580.3 25.3 %collective-permute-start.42 = (bf16[6,768,128]{2,1,0:T(8,128)(2,1)S(1)}, bf16[6,768,128]{2,1,0:T(8,128)(2,1)}, u32[]{:S(2)}, u32[]{:S(2)}) collective-permute-start(bf16[6,768,128]{2,1,0:T(8,128)(2,1)S(1)} %copy-done.47), channel_id=1, source_target_pairs={{0,1},{1,0},{2,3},{3,2},{4,5},{5,4},{6,7},{7,6},{8,9},{9,8},{10,11... | collective-permute-start | bytes 3538952 | tf_op jit(solution)/shard_map/ppermute | solution.py:231
  591.8 30.0 %collective-permute-start.34 = (bf16[768,1024]{1,0:T(8,128)(2,1)}, bf16[768,1024]{1,0:T(8,128)(2,1)}, u32[]{:S(2)}, u32[]{:S(2)}) collective-permute-start(bf16[768,1024]{1,0:T(8,128)(2,1)} %get-tuple-element.85), channel_id=1, source_target_pairs={{0,1},{1,0},{2,3},{3,2},{4,5},{5,4},{6,7},{7,6},{8,9},{9,8},{10,11... | collective-permute-start | bytes 4718600 | tf_op jit(solution)/shard_map/ppermute | solution.py:231
  593.0 30.4 %collective-permute-start.38 = (bf16[768,1024]{1,0:T(8,128)(2,1)}, bf16[768,1024]{1,0:T(8,128)(2,1)}, u32[]{:S(2)}, u32[]{:S(2)}) collective-permute-start(bf16[768,1024]{1,0:T(8,128)(2,1)} %get-tuple-element.79), channel_id=1, source_target_pairs={{0,1},{1,0},{2,3},{3,2},{4,5},{5,4},{6,7},{7,6},{8,9},{9,8},{10,11... | collective-permute-start | bytes 4718600 | tf_op jit(solution)/shard_map/ppermute | solution.py:231
  593.0 58.8 %collective-permute-start.50 = (bf16[1024,768]{1,0:T(8,128)(2,1)}, bf16[1024,768]{1,0:T(8,128)(2,1)}, u32[]{:S(2)}, u32[]{:S(2)}) collective-permute-start(bf16[1024,768]{1,0:T(8,128)(2,1)} %get-tuple-element.73), channel_id=1, source_target_pairs={{0,1},{1,0},{2,3},{3,2},{4,5},{5,4},{6,7},{7,6},{8,9},{9,8},{10,11... | collective-permute-start | bytes 4718600 | tf_op jit(solution)/shard_map/ppermute | solution.py:231
  610.7 43.8 %collective-permute-start.43 = (bf16[3,1536,128]{2,1,0:T(8,128)(2,1)}, bf16[3,1536,128]{2,1,0:T(8,128)(2,1)}, u32[]{:S(2)}, u32[]{:S(2)}) collective-permute-start(bf16[3,1536,128]{2,1,0:T(8,128)(2,1)} %pad_maximum_fusion.21), channel_id=1, source_target_pairs={{0,2},{1,3},{2,0},{3,1},{4,6},{5,7},{6,4},{7,5},{8,10},{9,11},{10,... | collective-permute-start | bytes 3538952 | tf_op jit(solution)/shard_map/ppermute | solution.py:218
  620.6 25.5 %collective-permute-start.64 = (bf16[128,1536]{1,0:T(8,128)(2,1)S(1)}, bf16[128,1536]{1,0:T(8,128)(2,1)S(1)}, u32[]{:S(2)}, u32[]{:S(2)}) collective-permute-start(bf16[128,1536]{1,0:T(8,128)(2,1)S(1)} %fusion.7), channel_id=1, source_target_pairs={{0,2},{1,3},{2,0},{3,1},{4,6},{5,7},{6,4},{7,5},{8,10},{9,11},{10,... | collective-permute-start | bytes 1179656 | tf_op jit(solution)/shard_map/ppermute | solution.py:218
  621.8 38.2 %collective-permute-start.49 = (bf16[4,768,256]{2,1,0:T(8,128)(2,1)}, bf16[4,768,256]{2,1,0:T(8,128)(2,1)}, u32[]{:S(2)}, u32[]{:S(2)}) collective-permute-start(bf16[4,768,256]{2,1,0:T(8,128)(2,1)} %pad_maximum_fusion.13), channel_id=1, source_target_pairs={{0,1},{1,0},{2,3},{3,2},{4,5},{5,4},{6,7},{7,6},{8,9},{9,8},{10,11... | collective-permute-start | bytes 4718600 | tf_op jit(solution)/shard_map/ppermute | solution.py:231
  623.4 33.0 %collective-permute-start.44 = (bf16[3,1536,128]{2,1,0:T(8,128)(2,1)}, bf16[3,1536,128]{2,1,0:T(8,128)(2,1)}, u32[]{:S(2)}, u32[]{:S(2)}) collective-permute-start(bf16[3,1536,128]{2,1,0:T(8,128)(2,1)} %pad_maximum_fusion.20.refs_8_), channel_id=1, source_target_pairs={{0,6},{1,7},{2,4},{3,5},{4,2},{5,3},{6,0},{7,1},{8,14},{9,15},{10,... | collective-permute-start | bytes 3538952 | tf_op jit(solution)/shard_map/ppermute | solution.py:218
  648.9 379.3 %all-gather.25.cloned.1.call-start = ((), (), s32[]{:S(2)}) async-start(), calls=%async_computation.17 | async-start | bytes 3932160 | tf_op jit(solution)/shard_map/all_gather | solution.py:299
  651.8 27.6 %collective-permute-start.55 = (bf16[384,1536]{1,0:T(8,128)(2,1)S(1)}, bf16[384,1536]{1,0:T(8,128)(2,1)S(1)}, u32[]{:S(2)}, u32[]{:S(2)}) collective-permute-start(bf16[384,1536]{1,0:T(8,128)(2,1)S(1)} %copy-done.49), channel_id=1, source_target_pairs={{0,2},{1,3},{2,0},{3,1},{4,6},{5,7},{6,4},{7,5},{8,10},{9,11},{10,... | collective-permute-start | bytes 3538952 | tf_op jit(solution)/shard_map/ppermute | solution.py:218
  651.8 61.3 %collective-permute-start.35 = (bf16[1536,512]{1,0:T(8,128)(2,1)}, bf16[1536,512]{1,0:T(8,128)(2,1)}, u32[]{:S(2)}, u32[]{:S(2)}) collective-permute-start(bf16[1536,512]{1,0:T(8,128)(2,1)} %pad_maximum_fusion.10), channel_id=1, source_target_pairs={{0,2},{1,3},{2,0},{3,1},{4,6},{5,7},{6,4},{7,5},{8,10},{9,11},{10,... | collective-permute-start | bytes 4718600 | tf_op jit(solution)/shard_map/ppermute | solution.py:218
  654.5 92.3 %collective-permute-start.39 = (bf16[1536,512]{1,0:T(8,128)(2,1)}, bf16[1536,512]{1,0:T(8,128)(2,1)}, u32[]{:S(2)}, u32[]{:S(2)}) collective-permute-start(bf16[1536,512]{1,0:T(8,128)(2,1)} %pad_maximum_fusion.12), channel_id=1, source_target_pairs={{0,2},{1,3},{2,0},{3,1},{4,6},{5,7},{6,4},{7,5},{8,10},{9,11},{10,... | collective-permute-start | bytes 4718600 | tf_op jit(solution)/shard_map/ppermute | solution.py:218
  656.4 90.4 %collective-permute-start.36 = (bf16[1536,512]{1,0:T(8,128)(2,1)}, bf16[1536,512]{1,0:T(8,128)(2,1)}, u32[]{:S(2)}, u32[]{:S(2)}) collective-permute-start(bf16[1536,512]{1,0:T(8,128)(2,1)} %pad_maximum_fusion.9.refs_0_), channel_id=1, source_target_pairs={{0,6},{1,7},{2,4},{3,5},{4,2},{5,3},{6,0},{7,1},{8,14},{9,15},{10,... | collective-permute-start | bytes 4718600 | tf_op jit(solution)/shard_map/ppermute | solution.py:218
  660.0 92.6 %collective-permute-start.40 = (bf16[1536,512]{1,0:T(8,128)(2,1)}, bf16[1536,512]{1,0:T(8,128)(2,1)}, u32[]{:S(2)}, u32[]{:S(2)}) collective-permute-start(bf16[1536,512]{1,0:T(8,128)(2,1)} %pad_maximum_fusion.11.refs_4_), channel_id=1, source_target_pairs={{0,6},{1,7},{2,4},{3,5},{4,2},{5,3},{6,0},{7,1},{8,14},{9,15},{10,... | collective-permute-start | bytes 4718600 | tf_op jit(solution)/shard_map/ppermute | solution.py:218
  679.4 167.2 %collective-permute-start.33 = (bf16[4,256,1536]{2,1,0:T(8,128)(2,1)}, bf16[4,256,1536]{2,1,0:T(8,128)(2,1)}, u32[]{:S(2)}, u32[]{:S(2)}) collective-permute-start(bf16[4,256,1536]{2,1,0:T(8,128)(2,1)} %bitcast.255), channel_id=1, source_target_pairs={{0,1},{1,0},{2,3},{3,2},{4,5},{5,4},{6,7},{7,6},{8,9},{9,8},{10,11... | collective-permute-start | bytes 9437192 | tf_op jit(solution)/shard_map/ppermute | solution.py:231
  713.1 39.9 %collective-permute-start.71 = (bf16[128,1536]{1,0:T(8,128)(2,1)}, bf16[128,1536]{1,0:T(8,128)(2,1)}, u32[]{:S(2)}, u32[]{:S(2)}) collective-permute-start(bf16[128,1536]{1,0:T(8,128)(2,1)} %slice_bitcast_fusion.10), channel_id=1, source_target_pairs={{0,6},{1,7},{2,4},{3,5},{4,2},{5,3},{6,0},{7,1},{8,14},{9,15},{10,... | collective-permute-start | bytes 1179656 | tf_op jit(solution)/shard_map/ppermute | solution.py:218
  746.8 35.4 %collective-permute-start.51 = (bf16[512,1536]{1,0:T(8,128)(2,1)}, bf16[512,1536]{1,0:T(8,128)(2,1)}, u32[]{:S(2)}, u32[]{:S(2)}) collective-permute-start(bf16[512,1536]{1,0:T(8,128)(2,1)} %pad_maximum_fusion.15), channel_id=1, source_target_pairs={{0,2},{1,3},{2,0},{3,1},{4,6},{5,7},{6,4},{7,5},{8,10},{9,11},{10,... | collective-permute-start | bytes 4718600 | tf_op jit(solution)/shard_map/ppermute | solution.py:218
  746.8 63.9 %collective-permute-start.37 = (bf16[1536,512]{1,0:T(8,128)(2,1)}, bf16[1536,512]{1,0:T(8,128)(2,1)}, u32[]{:S(2)}, u32[]{:S(2)}) collective-permute-start(bf16[1536,512]{1,0:T(8,128)(2,1)} %collective-permute-done.35.refs_1_), channel_id=1, source_target_pairs={{0,6},{1,7},{2,4},{3,5},{4,2},{5,3},{6,0},{7,1},{8,14},{9,15},{10,... | collective-permute-start | bytes 4718600 | tf_op jit(solution)/shard_map/ppermute | solution.py:218
  752.6 55.7 %collective-permute-start.45 = (bf16[3,1536,128]{2,1,0:T(8,128)(2,1)}, bf16[3,1536,128]{2,1,0:T(8,128)(2,1)S(1)}, u32[]{:S(2)}, u32[]{:S(2)}) collective-permute-start(bf16[3,1536,128]{2,1,0:T(8,128)(2,1)} %collective-permute-done.43.refs_9_), channel_id=1, source_target_pairs={{0,6},{1,7},{2,4},{3,5},{4,2},{5,3},{6,0},{7,1},{8,14},{9,15},{10,... | collective-permute-start | bytes 3538952 | tf_op jit(solution)/shard_map/ppermute | solution.py:218
  753.0 89.0 %collective-permute-start.41 = (bf16[1536,512]{1,0:T(8,128)(2,1)}, bf16[1536,512]{1,0:T(8,128)(2,1)S(1)}, u32[]{:S(2)}, u32[]{:S(2)}) collective-permute-start(bf16[1536,512]{1,0:T(8,128)(2,1)} %collective-permute-done.39.refs_5_), channel_id=1, source_target_pairs={{0,6},{1,7},{2,4},{3,5},{4,2},{5,3},{6,0},{7,1},{8,14},{9,15},{10,... | collective-permute-start | bytes 4718600 | tf_op jit(solution)/shard_map/ppermute | solution.py:218
  782.2 152.5 %collective-permute-start.52 = (bf16[512,1536]{1,0:T(8,128)(2,1)}, bf16[512,1536]{1,0:T(8,128)(2,1)}, u32[]{:S(2)}, u32[]{:S(2)}) collective-permute-start(bf16[512,1536]{1,0:T(8,128)(2,1)} %pad_maximum_fusion.14.refs_0_), channel_id=1, source_target_pairs={{0,6},{1,7},{2,4},{3,5},{4,2},{5,3},{6,0},{7,1},{8,14},{9,15},{10,... | collective-permute-start | bytes 4718600 | tf_op jit(solution)/shard_map/ppermute | solution.py:218
  808.4 151.8 %collective-permute-start.53 = (bf16[512,1536]{1,0:T(8,128)(2,1)}, bf16[512,1536]{1,0:T(8,128)(2,1)}, u32[]{:S(2)}, u32[]{:S(2)}) collective-permute-start(bf16[512,1536]{1,0:T(8,128)(2,1)} %collective-permute-done.51.refs_1_), channel_id=1, source_target_pairs={{0,6},{1,7},{2,4},{3,5},{4,2},{5,3},{6,0},{7,1},{8,14},{9,15},{10,... | collective-permute-start | bytes 4718600 | tf_op jit(solution)/shard_map/ppermute | solution.py:218
  810.7 33.7 %collective-permute-start.72 = (bf16[128,1536]{1,0:T(8,128)(2,1)S(1)}, bf16[128,1536]{1,0:T(8,128)(2,1)S(1)}, u32[]{:S(2)}, u32[]{:S(2)}) collective-permute-start(bf16[128,1536]{1,0:T(8,128)(2,1)S(1)} %fusion.3), channel_id=1, source_target_pairs={{0,2},{1,3},{2,0},{3,1},{4,6},{5,7},{6,4},{7,5},{8,10},{9,11},{10,... | collective-permute-start | bytes 1179656 | tf_op jit(solution)/shard_map/ppermute | solution.py:218
  842.1 92.7 %collective-permute-start.56 = (bf16[384,1536]{1,0:T(8,128)(2,1)S(1)}, bf16[384,1536]{1,0:T(8,128)(2,1)S(1)}, u32[]{:S(2)}, u32[]{:S(2)}) collective-permute-start(bf16[384,1536]{1,0:T(8,128)(2,1)S(1)} %pad_maximum_fusion.22.refs_4_), channel_id=1, source_target_pairs={{0,6},{1,7},{2,4},{3,5},{4,2},{5,3},{6,0},{7,1},{8,14},{9,15},{10,... | collective-permute-start | bytes 3538952 | tf_op jit(solution)/shard_map/ppermute | solution.py:218
  844.4 115.7 %collective-permute-start.57 = (bf16[384,1536]{1,0:T(8,128)(2,1)S(1)}, bf16[384,1536]{1,0:T(8,128)(2,1)}, u32[]{:S(2)}, u32[]{:S(2)}) collective-permute-start(bf16[384,1536]{1,0:T(8,128)(2,1)S(1)} %collective-permute-done.55.refs_5_), channel_id=1, source_target_pairs={{0,6},{1,7},{2,4},{3,5},{4,2},{5,3},{6,0},{7,1},{8,14},{9,15},{10,... | collective-permute-start | bytes 3538952 | tf_op jit(solution)/shard_map/ppermute | solution.py:218
  846.5 246.8 %reduce-scatter.9.cloned.1.call-start = ((), (), s32[]{:S(2)}) async-start(), calls=%async_computation.7 | async-start | bytes 3932160 | tf_op jit(solution)/shard_map/reduce_scatter | solution.py:307
  986.3 108.8 %reduce-scatter.13.cloned.1.call-start = ((), (), s32[]{:S(2)}) async-start(), calls=%async_computation.9 | async-start | bytes 3932160 | tf_op jit(solution)/shard_map/reduce_scatter | solution.py:307
  1039.2 90.1 %reduce-scatter.17.cloned.1.call-start = ((), (), s32[]{:S(2)}) async-start(), calls=%async_computation.11 | async-start | bytes 3932160 | tf_op jit(solution)/shard_map/reduce_scatter | solution.py:307
  1094.4 37.3 %collective-permute-start.59 = (bf16[128,1536]{1,0:T(8,128)(2,1)S(1)}, bf16[128,1536]{1,0:T(8,128)(2,1)S(1)}, u32[]{:S(2)}, u32[]{:S(2)}) collective-permute-start(bf16[128,1536]{1,0:T(8,128)(2,1)S(1)} %slice_bitcast_fusion.16), channel_id=1, source_target_pairs={{0,2},{1,3},{2,0},{3,1},{4,6},{5,7},{6,4},{7,5},{8,10},{9,11},{10,... | collective-permute-start | bytes 1179656 | tf_op jit(solution)/shard_map/ppermute | solution.py:218
  1096.2 36.6 %collective-permute-start.67 = (bf16[128,1536]{1,0:T(8,128)(2,1)S(1)}, bf16[128,1536]{1,0:T(8,128)(2,1)S(1)}, u32[]{:S(2)}, u32[]{:S(2)}) collective-permute-start(bf16[128,1536]{1,0:T(8,128)(2,1)S(1)} %slice_bitcast_fusion.12), channel_id=1, source_target_pairs={{0,2},{1,3},{2,0},{3,1},{4,6},{5,7},{6,4},{7,5},{8,10},{9,11},{10,... | collective-permute-start | bytes 1179656 | tf_op jit(solution)/shard_map/ppermute | solution.py:218
  (111 other events, 1579.7 us)
Sparse Core Ops, SparseCore 0:
  21.8 40.7 all-gather.14
  68.9 37.3 all-gather.18
  214.2 41.7 all-gather.22
  446.8 35.8 reduce-scatter.6
  498.7 35.8 reduce-scatter.10
  536.0 36.5 all-gather.16
  579.2 35.9 reduce-scatter.14
  649.0 38.8 all-gather.20
  846.7 42.0 all-gather.24
  986.5 37.9 reduce-scatter.8
  1039.4 38.0 reduce-scatter.12
  1091.2 38.0 reduce-scatter.16
